TPU v7x, 16 devices: a whole 2x2x2 slice. The times are simulated.
16 devices in a mesh: dp: 4 (over z, y), tp: 4 (over x, core).
Axes of the slice: x: 2, y: 2, z: 2, core: 2. Of those that a mesh axis runs over, the one named last changes fastest.
Arguments:
- hidden: bfloat16 [512, 2048], P('dp'), parts along dimension 0
- seq_lens: int32 [512], P('dp'), parts along dimension 0
- k_cache: bfloat16 [2, 512, 256, 8, 64], P(None, 'dp', None, 'tp'), parts along dimension 1
- v_cache: bfloat16 [2, 512, 256, 8, 64], P(None, 'dp', None, 'tp'), parts along dimension 1
- g_attn: bfloat16 [2, 2048], replicated
- w_q: bfloat16 [2, 2048, 2048], P(None, None, 'tp')
- w_k: bfloat16 [2, 2048, 512], P(None, None, 'tp')
- w_v: bfloat16 [2, 2048, 512], P(None, None, 'tp')
- w_o: bfloat16 [2, 2048, 2048], P(None, 'tp')
- g_mlp: bfloat16 [2, 2048], replicated
- w_gate: bfloat16 [2, 2048, 8192], P(None, None, 'tp')
- w_up: bfloat16 [2, 2048, 8192], P(None, None, 'tp')
- w_down: bfloat16 [2, 8192, 2048], P(None, 'tp')
Outputs:
- output 1: bfloat16 [512, 2048], P('dp'), parts along dimension 0
- output 2: bfloat16 [2, 512, 256, 8, 64], P(None, 'dp', None, 'tp'), parts along dimension 1
- output 3: bfloat16 [2, 512, 256, 8, 64], P(None, 'dp', None, 'tp'), parts along dimension 1
There are 4 independent parts. A program takes and returns all parts, laid end to end along the dimension named above; an argument that names none is the same for every part.
All inputs are finite; a program needn't handle non-finite values.
Results may differ from a plain program's by a relative error of at most 0.0171893.
Values are sent between devices in bfloat16 or wider.
A program may use at most 1 GiB of HBM per device.

v0:
```python
import jax
import jax.numpy as jnp
from jax import lax
from jax.sharding import PartitionSpec as P

NORM_EPS = 1e-5
ROPE_THETA = 500000.0
ROPE_FACTOR = 8.0
LOW_FACTOR = 1.0
HIGH_FACTOR = 4.0
ORIG_CONTEXT = 8192.0


def rope_freqs(head_dim):
    freq_expo = jnp.arange(0, head_dim, 2).astype(jnp.float32) / head_dim
    inv_freq = 1.0 / (ROPE_THETA ** freq_expo)
    wavelen = 2.0 * jnp.pi / inv_freq
    smooth = (ORIG_CONTEXT / wavelen - LOW_FACTOR) / (HIGH_FACTOR - LOW_FACTOR)
    blended = (1.0 - smooth) * inv_freq / ROPE_FACTOR + smooth * inv_freq
    return jnp.where(wavelen > ORIG_CONTEXT / LOW_FACTOR, inv_freq / ROPE_FACTOR,
                     jnp.where(wavelen < ORIG_CONTEXT / HIGH_FACTOR, inv_freq, blended))


def apply_rope(vectors, pos_angle):
    shaped = pos_angle.reshape(pos_angle.shape[:1] + (1,) * (vectors.ndim - 2) + pos_angle.shape[1:])
    cos_part = jnp.cos(shaped)
    sin_part = jnp.sin(shaped)
    half_dim = vectors.shape[-1] // 2
    lower_half = vectors[..., :half_dim]
    upper_half = vectors[..., half_dim:]
    return jnp.concatenate([lower_half * cos_part - upper_half * sin_part,
                            upper_half * cos_part + lower_half * sin_part], axis=-1)


def rms_norm(hidden, gain_vec):
    hidden_f = hidden.astype(jnp.float32)
    inv_rms = lax.rsqrt(jnp.mean(hidden_f * hidden_f, axis=-1, keepdims=True) + NORM_EPS)
    return (hidden_f * inv_rms * gain_vec.astype(jnp.float32)).astype(jnp.bfloat16)


def add_residual(hidden, delta):
    return (hidden.astype(jnp.float32) + delta.astype(jnp.float32)).astype(jnp.bfloat16)


def attend(q_rot, k_new, v_new, k_old, v_old, seq_lens):
    attn_scale = q_rot.shape[-1] ** -0.5
    old_scores = jnp.einsum("bkgh,bskh->bkgs", q_rot, k_old, preferred_element_type=jnp.float32) * attn_scale
    new_scores = jnp.einsum("bkgh,bkh->bkg", q_rot, k_new, preferred_element_type=jnp.float32) * attn_scale
    positions = jnp.arange(k_old.shape[1])
    visible = (positions[None, :] < seq_lens[:, None])[:, None, None, :]
    old_scores = jnp.where(visible, old_scores, -1e30)
    row_peak = jnp.maximum(jnp.max(old_scores, axis=-1), new_scores)
    old_exp = jnp.exp(old_scores - row_peak[..., None])
    new_exp = jnp.exp(new_scores - row_peak)
    row_denom = jnp.sum(old_exp, axis=-1) + new_exp
    prob_old = (old_exp / row_denom[..., None]).astype(jnp.bfloat16)
    prob_new = (new_exp / row_denom).astype(jnp.bfloat16)
    attn_mix = jnp.einsum("bkgs,bskh->bkgh", prob_old, v_old, preferred_element_type=jnp.float32)
    attn_mix = attn_mix + prob_new.astype(jnp.float32)[..., None] * v_new.astype(jnp.float32)[:, :, None, :]
    return attn_mix.astype(jnp.bfloat16)


def attention_block(normed, seq_lens, k_old, v_old, w_q, w_k, w_v):
    batch_rows = normed.shape[0]
    kv_heads = k_old.shape[2]
    head_dim = k_old.shape[3]
    groups = w_q.shape[1] // (kv_heads * head_dim)
    pos_angle = seq_lens.astype(jnp.float32)[:, None] * rope_freqs(head_dim)[None, :]
    q_full = jnp.dot(normed, w_q, preferred_element_type=jnp.float32).reshape(batch_rows, kv_heads, groups, head_dim)
    k_full = jnp.dot(normed, w_k, preferred_element_type=jnp.float32).reshape(batch_rows, kv_heads, head_dim)
    v_new = jnp.dot(normed, w_v, preferred_element_type=jnp.float32).reshape(batch_rows, kv_heads, head_dim).astype(jnp.bfloat16)
    q_rot = apply_rope(q_full, pos_angle).astype(jnp.bfloat16)
    k_new = apply_rope(k_full, pos_angle).astype(jnp.bfloat16)
    attn_out = attend(q_rot, k_new, v_new, k_old, v_old, seq_lens)
    return attn_out.reshape(batch_rows, kv_heads * groups * head_dim), k_new, v_new


def mlp_partial(normed, w_gate, w_up, w_down):
    gate_proj = jnp.dot(normed, w_gate, preferred_element_type=jnp.float32)
    up_proj = jnp.dot(normed, w_up, preferred_element_type=jnp.float32)
    mlp_act = (jax.nn.silu(gate_proj) * up_proj).astype(jnp.bfloat16)
    return jnp.dot(mlp_act, w_down, preferred_element_type=jnp.float32)


def write_cache(cache, new_rows, seq_lens):
    positions = jnp.arange(cache.shape[2])
    at_new = (positions[None, :] == seq_lens[:, None])[None, :, :, None, None]
    return jnp.where(at_new, new_rows[:, :, None], cache)


def solution(mesh):
    cache_spec = P(None, "dp", None, "tp", None)
    col_spec = P(None, None, "tp")
    row_spec = P(None, "tp", None)
    in_specs = (P("dp", None), P("dp"), cache_spec, cache_spec, P(None, None), col_spec, col_spec, col_spec,
                row_spec, P(None, None), col_spec, col_spec, row_spec)
    out_specs = (P("dp", None), cache_spec, cache_spec)

    def local_step(hidden, seq_lens, k_cache, v_cache, g_attn, w_q, w_k, w_v, w_o, g_mlp, w_gate, w_up, w_down):
        k_rows = []
        v_rows = []
        for layer_idx in range(k_cache.shape[0]):
            normed = rms_norm(hidden, g_attn[layer_idx])
            attn_out, k_new, v_new = attention_block(normed, seq_lens, k_cache[layer_idx], v_cache[layer_idx],
                                                     w_q[layer_idx], w_k[layer_idx], w_v[layer_idx])
            attn_part = jnp.dot(attn_out, w_o[layer_idx], preferred_element_type=jnp.float32).astype(jnp.bfloat16)
            hidden = add_residual(hidden, lax.psum(attn_part, "tp"))
            normed = rms_norm(hidden, g_mlp[layer_idx])
            mlp_part = mlp_partial(normed, w_gate[layer_idx], w_up[layer_idx], w_down[layer_idx]).astype(jnp.bfloat16)
            hidden = add_residual(hidden, lax.psum(mlp_part, "tp"))
            k_rows.append(k_new)
            v_rows.append(v_new)
        k_out = write_cache(k_cache, jnp.stack(k_rows), seq_lens)
        v_out = write_cache(v_cache, jnp.stack(v_rows), seq_lens)
        return hidden, k_out, v_out

    return jax.shard_map(local_step, mesh=mesh, in_specs=in_specs, out_specs=out_specs, check_vma=False)
```

profile of v0, /device:TPU:0, one launch (start us, length us, event | category | flops | bytes accessed | tf_op | source)
XLA Modules:
  0.0 222.2 jit_solution(12414954403274490073)
XLA Ops:
  12.2 2.1 slice_bitcast_fusion.2
  14.5 1.4 fusion.106
  15.9 1.4 convolution_convert_fusion.3
  17.5 3.8 %slice_bitcast_fusion.1 = (bf16[512,2048]{0,1:T(8,128)(2,1)S(1)}, bf16[512,2048]{0,1:T(8,128)(2,1)}) fusion(bf16[2,2048,512]{2,1,0:T(8,128)(2,1)} %param.18), kind=kLoop, calls=%fused_computation.45 | loop fusion | bytes 8388608 | tf_op jit(solution)/shard_map/dot_general | solution.py:69
  21.3 2.4 %copy.62 = bf16[512,2048]{1,0:T(8,128)(2,1)} copy(bf16[512,2048]{0,1:T(8,128)(2,1)S(1)} %get-tuple-element.7) | data formatting | bytes 4194304 | tf_op jit(solution)/shard_map/dot_general | solution.py:69
  23.7 2.4 %fusion.100 = f32[128,2,4,64]{0,3,2,1:T(8,128)S(1)} fusion(bf16[2,4,64,2048]{3,2,1,0:T(8,128)(2,1)} %bitcast.149, bf16[128,2048]{1,0:T(8,128)(2,1)S(1)} %copy-done.1, f32[2048]{0:T(1024)S(1)} %bitcast.167, f32[128]{0:T(128)S(1)} %add_rsqrt_fusion.3), kind=kOutput, calls=%fused_computation.92 | convolution fusion | flops 269484032 | bytes 2892288 | tf_op jit(solution)/shard_map/dot_general | solution.py:69
  26.5 4.8 %fusion.131 = (f32[128,2,4]{2,1,0:T(2,128)S(1)}, f32[128,2,4,256]{3,2,1,0:T(4,128)S(1)}) fusion(bf16[128,2,4,64]{3,2,1,0:T(4,128)(2,1)S(1)} %copy.63, bf16[2,128,256,2,64]{2,4,3,1,0:T(8,128)(2,1)} %param.15, pred[128,256]{1,0:T(8,128)(4,1)S(1)} %get-tuple-element.34), kind=kOutput, calls=%fused_computation.152 | convolution fusion | flops 34339840 | bytes 9605120 | tf_op jit(solution)/shard_map/bkgh,bskh->bkgs/dot_general | solution.py:47
  32.9 4.7 %fusion.67 = bf16[128,2,4,64]{3,2,1,0:T(4,128)(2,1)S(1)} fusion(bf16[2,128,256,2,64]{2,4,3,1,0:T(8,128)(2,1)} %param.16, f32[128,2,4,256]{3,2,1,0:T(4,128)S(1)} %get-tuple-element.36, f32[128,2,4]{2,1,0:T(2,128)S(1)} %copy.68, f32[128,2,4]{2,1,0:T(2,128)S(1)} %copy.66, f32[128,2,64]{2,1,0:T(2,128)S(1)} %copy.71, f32[128,2,4]{2,1,0:T(2,128)S(1)} %copy.69), kind=kOutput, calls=%fused_computation.63 | convolution fusion | flops 34537472 | bytes 9646080 | tf_op jit(solution)/shard_map/bkgs,bskh->bkgh/dot_general | solution.py:58
  37.9 2.9 %convolution_convert_fusion.1 = bf16[128,2048]{1,0:T(8,128)(2,1)} fusion(bf16[128,512]{0,1:T(8,128)(2,1)S(1)} %bitcast.154, bf16[2,512,2048]{2,1,0:T(8,128)(2,1)} %param.21), kind=kOutput, calls=%fused_computation.39 | convolution fusion | flops 268697600 | bytes 2752512 | tf_op jit(solution)/shard_map/dot_general | solution.py:106
  40.8 32.5 %all-reduce.5.cloned.1.call-done = bf16[128,2048]{1,0:T(8,128)(2,1)} async-done(((bf16[128,2048]{1,0:T(8,128)(2,1)}), bf16[128,2048]{1,0:T(8,128)(2,1)}) %all-reduce.5.cloned.1.call-update) | async-done | bytes 524304 | tf_op jit(solution)/shard_map/psum | solution.py:107
  74.6 4.7 %fusion.14 = f32[128,2048]{1,0:T(8,128)S(1)} fusion(bf16[2,2048,2048]{2,1,0:T(8,128)(2,1)} %param.23, bf16[128,2048]{1,0:T(8,128)(2,1)S(1)} %get-tuple-element.6, f32[2048]{0:T(1024)S(1)} %bitcast.168, f32[128]{0:T(128)S(1)} %add_rsqrt_fusion.2), kind=kOutput, calls=%fused_computation.16 | convolution fusion | flops 1074790400 | bytes 9970176 | tf_op jit(solution)/shard_map/dot_general | solution.py:79
  79.3 9.2 %fusion.36 = bf16[128,2048]{1,0:T(8,128)(2,1)} fusion(bf16[2,2048,2048]{2,1,0:T(8,128)(2,1)} %param.25, bf16[2,2048,2048]{2,1,0:T(8,128)(2,1)} %param.24, f32[128,2048]{1,0:T(8,128)S(1)} %fusion.14, bf16[128,2048]{1,0:T(8,128)(2,1)S(1)} %get-tuple-element.6, f32[2048]{0:T(1024)S(1)} %bitcast.169, f32[128]{0:T(128)S(1)} %add_rsqrt_fusion.2), kind=kOutput, calls=%fused_computation.34 | convolution fusion | flops 2150367232 | bytes 18883072 | tf_op jit(solution)/shard_map/dot_general | solution.py:82
  90.8 2.9 %copy.73 = bf16[512,2048]{1,0:T(8,128)(2,1)S(1)} copy(bf16[512,2048]{0,1:T(8,128)(2,1)} %get-tuple-element.8) | data formatting | bytes 4194304 | tf_op jit(solution)/shard_map/dot_general | solution.py:69
  93.8 24.5 %all-reduce.7.cloned.1.call-done = bf16[128,2048]{1,0:T(8,128)(2,1)} async-done(((bf16[128,2048]{1,0:T(8,128)(2,1)}), bf16[128,2048]{1,0:T(8,128)(2,1)}) %all-reduce.7.cloned.1.call-update) | async-done | bytes 524304 | tf_op jit(solution)/shard_map/psum | solution.py:110
  124.7 4.8 %fusion.132 = (f32[128,2,4]{2,1,0:T(2,128)S(1)}, f32[128,2,4,256]{3,2,1,0:T(4,128)S(1)}) fusion(bf16[128,2,4,64]{3,2,1,0:T(4,128)(2,1)S(1)} %copy.74, bf16[2,128,256,2,64]{2,4,3,1,0:T(8,128)(2,1)} %param.15, pred[128,256]{1,0:T(8,128)(4,1)S(1)} %copy-done.4), kind=kOutput, calls=%fused_computation.153 | convolution fusion | flops 34339840 | bytes 9605120 | tf_op jit(solution)/shard_map/bkgh,bskh->bkgs/dot_general | solution.py:47
  131.1 4.8 %fusion.64 = bf16[128,2,4,64]{3,2,1,0:T(4,128)(2,1)S(1)} fusion(bf16[2,128,256,2,64]{2,4,3,1,0:T(8,128)(2,1)} %param.16, f32[128,2,4,256]{3,2,1,0:T(4,128)S(1)} %get-tuple-element.38, f32[128,2,4]{2,1,0:T(2,128)S(1)} %copy.79, f32[128,2,4]{2,1,0:T(2,128)S(1)} %copy.77, f32[128,2,64]{2,1,0:T(2,128)S(1)} %copy.82, f32[128,2,4]{2,1,0:T(2,128)S(1)} %copy.80), kind=kOutput, calls=%fused_computation.62 | convolution fusion | flops 34537472 | bytes 9646080 | tf_op jit(solution)/shard_map/bkgs,bskh->bkgh/dot_general | solution.py:58
  136.1 2.9 %convolution_convert_fusion = bf16[128,2048]{1,0:T(8,128)(2,1)} fusion(bf16[128,512]{0,1:T(8,128)(2,1)S(1)} %bitcast.155, bf16[2,512,2048]{2,1,0:T(8,128)(2,1)} %param.21), kind=kOutput, calls=%fused_computation.38 | convolution fusion | flops 268697600 | bytes 2752512 | tf_op jit(solution)/shard_map/dot_general | solution.py:106
  139.3 29.4 %all-reduce.9.cloned.1.call-done = bf16[128,2048]{1,0:T(8,128)(2,1)} async-done(((bf16[128,2048]{1,0:T(8,128)(2,1)}), bf16[128,2048]{1,0:T(8,128)(2,1)}) %all-reduce.9.cloned.1.call-update) | async-done | bytes 524304 | tf_op jit(solution)/shard_map/psum | solution.py:107
  168.7 1.4 fusion.88
  170.1 4.7 %fusion.4 = f32[128,2048]{1,0:T(8,128)S(1)} fusion(bf16[2,2048,2048]{2,1,0:T(8,128)(2,1)} %param.23, bf16[128,2048]{1,0:T(8,128)(2,1)S(1)} %get-tuple-element.4, f32[2048]{0:T(1024)S(1)} %bitcast.163, f32[128]{0:T(128)S(1)} %add_rsqrt_fusion), kind=kOutput, calls=%fused_computation.6 | convolution fusion | flops 1074790400 | bytes 9970176 | tf_op jit(solution)/shard_map/dot_general | solution.py:79
  174.8 9.2 %fusion.39 = bf16[128,2048]{1,0:T(8,128)(2,1)} fusion(bf16[2,2048,2048]{2,1,0:T(8,128)(2,1)} %param.25, bf16[2,2048,2048]{2,1,0:T(8,128)(2,1)} %param.24, f32[128,2048]{1,0:T(8,128)S(1)} %fusion.4, bf16[128,2048]{1,0:T(8,128)(2,1)S(1)} %get-tuple-element.4, f32[2048]{0:T(1024)S(1)} %bitcast.164, f32[128]{0:T(128)S(1)} %add_rsqrt_fusion), kind=kOutput, calls=%fused_computation.35 | convolution fusion | flops 2150367232 | bytes 18883072 | tf_op jit(solution)/shard_map/dot_general | solution.py:82
  184.0 23.0 %broadcast_select_fusion = (bf16[2,128,256,2,64]{2,4,3,1,0:T(8,128)(2,1)}, bf16[2,128,256,2,64]{2,4,3,1,0:T(8,128)(2,1)}) fusion(bf16[2,128,256,2,64]{2,4,3,1,0:T(8,128)(2,1)} %param.16, pred[128,256]{1,0:T(8,128)(4,1)S(1)} %get-tuple-element.33, bf16[2,128,2,64]{3,2,1,0:T(2,128)(2,1)S(1)} %copy.85, bf16[2,128,256,2,64]{2,4,3,1,0:T(8,128)(2,1)} %param.15, ...), kind=kLoop, calls=%fused_computation | loop fusion | flops 16777216 | bytes 67272704 | tf_op jit(solution)/shard_map/jit(_where)/select_n | solution.py:88
  206.9 6.7 %all-reduce.11.cloned.1.call-done = bf16[128,2048]{1,0:T(8,128)(2,1)} async-done(((bf16[128,2048]{1,0:T(8,128)(2,1)}), bf16[128,2048]{1,0:T(8,128)(2,1)}) %all-reduce.11.cloned.1.call-update) | async-done | bytes 524304 | tf_op jit(solution)/shard_map/psum | solution.py:110
  213.7 2.0 fusion.91
  (78 shorter events, 19.7 us)
Async XLA Ops:
  7.2 66.1 %all-reduce.5.cloned.1.call-start = ((), (), s32[]{:S(2)}) async-start(), calls=%async_computation | async-start | bytes 1048576 | tf_op jit(solution)/shard_map/psum | solution.py:107
  8.7 17.9 %copy-start.3 = (pred[128,256]{1,0:T(8,128)(4,1)}, pred[128,256]{1,0:T(8,128)(4,1)S(1)}, u32[]{:S(2)}) copy-start(pred[128,256]{1,0:T(8,128)(4,1)S(1)} %get-tuple-element.34) | copy-start | bytes 98308
  14.3 9.4 %copy-start.1 = (bf16[128,2048]{1,0:T(8,128)(2,1)S(1)}, bf16[128,2048]{1,0:T(8,128)(2,1)}, u32[]{:S(2)}) copy-start(bf16[128,2048]{1,0:T(8,128)(2,1)} %param.13) | copy-start | bytes 1572868
  32.9 7.9 %copy-start.5 = (bf16[2,2048]{1,0:T(2,128)(2,1)S(1)}, bf16[2,2048]{1,0:T(2,128)(2,1)}, u32[]{:S(2)}) copy-start(bf16[2,2048]{1,0:T(2,128)(2,1)} %param.22) | copy-start | bytes 24580
  40.8 77.5 %all-reduce.7.cloned.1.call-start = ((), (), s32[]{:S(2)}) async-start(), calls=%async_computation.1 | async-start | bytes 1048576 | tf_op jit(solution)/shard_map/psum | solution.py:110
  79.3 10.5 %copy-start.2 = (bf16[128,2048]{0,1:T(8,128)(2,1)S(1)}, bf16[128,2048]{0,1:T(8,128)(2,1)}, u32[]{:S(2)}) copy-start(bf16[128,2048]{0,1:T(8,128)(2,1)} %get-tuple-element.9) | copy-start | bytes 1572868
  88.5 36.2 %copy-start.4 = (pred[128,256]{1,0:T(8,128)(4,1)S(1)}, pred[128,256]{1,0:T(8,128)(4,1)}, u32[]{:S(2)}) copy-start(pred[128,256]{1,0:T(8,128)(4,1)} %copy-done.3) | copy-start | bytes 98308
  88.6 80.1 %all-reduce.9.cloned.1.call-start = ((), (), s32[]{:S(2)}) async-start(), calls=%async_computation.2 | async-start | bytes 1048576 | tf_op jit(solution)/shard_map/psum | solution.py:107
  131.1 37.6 %copy-start = (bf16[128,2048]{1,0:T(8,128)(2,1)S(1)}, bf16[128,2048]{1,0:T(8,128)(2,1)}, u32[]{:S(2)}) copy-start(bf16[128,2048]{1,0:T(8,128)(2,1)} %all-reduce.7.cloned.1.call-done) | copy-start | bytes 1572868
  139.0 74.7 %all-reduce.11.cloned.1.call-start = ((), (), s32[]{:S(2)}) async-start(), calls=%async_computation.3 | async-start | bytes 1048576 | tf_op jit(solution)/shard_map/psum | solution.py:110
Sparse Core Ops, SparseCore 0:
  40.9 32.3 all-reduce.4
  88.7 29.5 all-reduce.6
  139.1 29.5 all-reduce.8
  184.1 29.5 all-reduce.10
where the time goes:
time: 223 us; the launch traced here: 222 us
  waiting for transfers between devices  93.1 us (42%)
  matrix products  61.2 us (27%)
  other arithmetic  35.9 us (16%)
  local copies, waits for them, and re-layouts  17.5 us (8%)
  between operations  14.2 us (6%)
    psum x2, waiting for transfers between devices, local_step(): hidden = add_residual(hidden, lax.psum(attn_part, 'tp'))  61.8 us
    psum x2, waiting for transfers between devices, local_step(): hidden = add_residual(hidden, lax.psum(mlp_part, 'tp'))  31.2 us
    select_n x1, other arithmetic, write_cache(): return jnp.where(at_new, new_rows[:, :, None], cache)  23 us
    dot_general x2, matrix products, mlp_partial(): return jnp.dot(mlp_act, w_down, preferred_element_type=jnp.float32)  18.4 us
    dot_general x2, matrix products, attend(): jnp.einsum('bkgh,bskh->bkgs', q_rot, k_old, preferred_element_type=jnp.fl...  9.58 us
    dot_general x2, matrix products, attend(): jnp.einsum('bkgs,bskh->bkgh', prob_old, v_old, preferred_element_type=jnp...  9.51 us
    dot_general x2, matrix products, mlp_partial(): gate_proj = jnp.dot(normed, w_gate, preferred_element_type=jnp.float32)  9.38 us
    dot_general x3, local copies, waits for them, and re-layouts, attention_block(): jnp.dot(normed, w_q, preferred_element_type=jnp.float32)  9.1 us
  transfers between devices with their start and end apart: 4, of which 4 were waited for; matrix products, arithmetic and copies ran while one was open for 13% of the time, Pallas kernels for 0%

commit v1 on v0

v1 whole, which is shorter than its diff:
```python
import functools

import jax
import jax.numpy as jnp
from jax import lax
from jax.experimental import pallas as pl
from jax.experimental.pallas import tpu as pltpu
from jax.sharding import PartitionSpec as P

NORM_EPS = 1e-5
ROPE_THETA = 500000.0
ROPE_FACTOR = 8.0
LOW_FACTOR = 1.0
HIGH_FACTOR = 4.0
ORIG_CONTEXT = 8192.0

ROWS = 128
D = 2048
SMAX = 256
HEAD = 64
KVD = 128
QD = 512
FF = 2048
SEQS = 8
STEPS = ROWS // SEQS
CW = 512
NCH = D // CW
F32 = jnp.float32
BF16 = jnp.bfloat16
MESH = pl.DeviceIdType.MESH
ANY = pl.BlockSpec(memory_space=pl.ANY)
VMEM = pl.BlockSpec(memory_space=pltpu.VMEM)
SMEM = pl.BlockSpec(memory_space=pltpu.SMEM)


def rope_freqs(head_dim):
    freq_expo = jnp.arange(0, head_dim, 2).astype(F32) / head_dim
    inv_freq = 1.0 / (ROPE_THETA ** freq_expo)
    wavelen = 2.0 * jnp.pi / inv_freq
    smooth = (ORIG_CONTEXT / wavelen - LOW_FACTOR) / (HIGH_FACTOR - LOW_FACTOR)
    blended = (1.0 - smooth) * inv_freq / ROPE_FACTOR + smooth * inv_freq
    return jnp.where(wavelen > ORIG_CONTEXT / LOW_FACTOR, inv_freq / ROPE_FACTOR,
                     jnp.where(wavelen < ORIG_CONTEXT / HIGH_FACTOR, inv_freq, blended))


def norm_rows(hidden_f, gain):
    inv_rms = lax.rsqrt(jnp.mean(hidden_f * hidden_f, axis=-1, keepdims=True) + NORM_EPS)
    return (hidden_f * inv_rms * gain.astype(F32)).astype(BF16)


def rope_slab(slab, cos, sin):
    lane = lax.broadcasted_iota(jnp.int32, slab.shape, 1)
    other = jnp.where(lane % HEAD < HEAD // 2, pltpu.roll(slab, 128 - HEAD // 2, 1), pltpu.roll(slab, HEAD // 2, 1))
    return slab * cos + other * sin


def attn_kernel(layer, aliased, *refs):
    if aliased:
        (seq_ref, h_ref, cos_ref, sin_ref, g_ref, wq_hbm, wk_hbm, wv_hbm, k_hbm, v_hbm, _, _,
         out_ref, ko_hbm, vo_hbm, wq, wk, wv, kbuf, vbuf, knew, vnew, qrow, orow, wsem, ksem, vsem, osem) = refs
    else:
        (seq_ref, h_ref, cos_ref, sin_ref, g_ref, wq_hbm, wk_hbm, wv_hbm, k_hbm, v_hbm,
         out_ref, ko_hbm, vo_hbm, wq, wk, wv, kbuf, vbuf, knew, vnew, qrow, orow, wsem, ksem, vsem, osem) = refs

    def load_w(i):
        src, dst = ((wk_hbm, wk), (wv_hbm, wv), (wq_hbm, wq))[i]
        return pltpu.make_async_copy(src.at[layer], dst, wsem.at[i])

    def load_k(i):
        return pltpu.make_async_copy(k_hbm.at[layer, pl.ds(i * SEQS, SEQS)], kbuf.at[pl.ds(i * SEQS, SEQS)], ksem.at[i])

    def load_v(i):
        return pltpu.make_async_copy(v_hbm.at[layer, pl.ds(i * SEQS, SEQS)], vbuf.at[pl.ds(i * SEQS, SEQS)], vsem.at[i])

    def store_k(i):
        return pltpu.make_async_copy(kbuf.at[pl.ds(i * SEQS, SEQS)], ko_hbm.at[layer, pl.ds(i * SEQS, SEQS)], osem.at[0, i])

    def store_v(i):
        return pltpu.make_async_copy(vbuf.at[pl.ds(i * SEQS, SEQS)], vo_hbm.at[layer, pl.ds(i * SEQS, SEQS)], osem.at[1, i])

    for i in range(3):
        load_w(i).start()
    for i in range(STEPS):
        load_k(i).start()
        load_v(i).start()

    normed = norm_rows(h_ref[...].astype(F32), g_ref[layer:layer + 1, :])
    cos = cos_ref[...]
    sin = sin_ref[...]
    load_w(0).wait()
    k_rot = rope_slab(jnp.dot(normed, wk[...], preferred_element_type=F32), cos, sin).astype(BF16).astype(F32).T
    load_w(1).wait()
    v_row = jnp.dot(normed, wv[...], preferred_element_type=F32).astype(BF16).astype(F32).T
    for i in range(STEPS):
        shift = (ROWS - i * SEQS) % ROWS
        knew[i] = (pltpu.roll(k_rot, shift, 1) if shift else k_rot).astype(BF16)
        vnew[i] = (pltpu.roll(v_row, shift, 1) if shift else v_row).astype(BF16)
    load_w(2).wait()
    lane = lax.broadcasted_iota(jnp.int32, (ROWS, 128), 1)
    for slab_idx in range(4):
        slab = jnp.dot(normed, wq[:, slab_idx * 128:(slab_idx + 1) * 128], preferred_element_type=F32)
        slab = rope_slab(slab, cos, sin).astype(BF16).astype(F32)
        turned = pltpu.roll(slab, HEAD, 1)
        for half in range(2):
            hg = slab_idx * 2 + half
            kv = hg // 4
            qrow[pl.ds(hg, ROWS, stride=8), :] = jnp.where(lane // HEAD == kv, slab if kv == half else turned, 0.0)

    def step(i, carry):
        load_k(i).wait()
        load_v(i).wait()
        lane16 = lax.broadcasted_iota(jnp.int16, (KVD, SMAX), 1)
        lane8 = lax.broadcasted_iota(jnp.int32, (8, SMAX), 1)
        row16 = lax.broadcasted_iota(jnp.int32, (16, 128), 0)
        row8 = lax.broadcasted_iota(jnp.int32, (8, 128), 0)
        lane_o = lax.broadcasted_iota(jnp.int32, (8, 128), 1)
        for j in range(SEQS):
            b = i * SEQS + j
            here = lane16 == seq_ref[b].astype(jnp.int16)
            kbuf[b] = jnp.where(here, jnp.broadcast_to(knew[i, :, j:j + 1], (KVD, SMAX)), kbuf[b])
            vbuf[b] = jnp.where(here, jnp.broadcast_to(vnew[i, :, j:j + 1], (KVD, SMAX)), vbuf[b])
        store_k(i).start()
        store_v(i).start()
        scores = []
        for p in range(SEQS // 2):
            b = i * SEQS + 2 * p
            q2 = qrow[pl.ds(b * 8, 16), :]
            qb = jnp.concatenate([jnp.where(row16 < 8, q2, 0.0), jnp.where(row16 >= 8, q2, 0.0)], axis=1).astype(BF16)
            kk = kbuf[pl.ds(b, 2)].reshape(2 * KVD, SMAX)
            scores.append(jnp.dot(qb, kk, preferred_element_type=F32) * (HEAD ** -0.5))
        for p in range(SEQS // 2):
            b = i * SEQS + 2 * p
            halves = []
            for j in range(2):
                s = jnp.where(lane8 <= seq_ref[b + j], scores[p][8 * j:8 * j + 8], -1e30)
                e = jnp.exp(s - jnp.max(s, axis=-1, keepdims=True))
                halves.append(e / jnp.sum(e, axis=-1, keepdims=True))
            prob = jnp.concatenate(halves, axis=0).astype(BF16)
            vv = vbuf[pl.ds(b, 2)].reshape(2 * KVD, SMAX)
            mix = lax.dot_general(prob, vv, (((1,), (1,)), ((), ())), preferred_element_type=F32)
            for j in range(2):
                m = mix[8 * j:8 * j + 8, 128 * j:128 * j + 128]
                orow[pl.ds((b + j) * 8, 8), :] = jnp.where((row8 < 4) == (lane_o < HEAD), m, pltpu.roll(m, HEAD, 1))
        return carry

    lax.fori_loop(0, STEPS, step, 0)
    for slab_idx in range(4):
        lower = orow[pl.ds(slab_idx * 2, ROWS, stride=8), :]
        upper = orow[pl.ds(slab_idx * 2 + 1, ROWS, stride=8), :]
        out_ref[:, slab_idx * 128:(slab_idx + 1) * 128] = jnp.where(lane < HEAD, lower, upper).astype(BF16)
    for i in range(STEPS):
        store_k(i).wait()
        store_v(i).wait()


def attn_call(layer, seq_lens, hidden, cos, sin, g_attn, w_q, w_k, w_v, k_cache, v_cache, outs=()):
    cache = jax.ShapeDtypeStruct(k_cache.shape, BF16)
    return pl.pallas_call(
        functools.partial(attn_kernel, layer, bool(outs)),
        out_shape=(jax.ShapeDtypeStruct((ROWS, QD), BF16), cache, cache),
        in_specs=[SMEM, VMEM, VMEM, VMEM, VMEM] + [ANY] * (5 + len(outs)),
        out_specs=(VMEM, ANY, ANY),
        scratch_shapes=[
            pltpu.VMEM((D, QD), BF16),
            pltpu.VMEM((D, KVD), BF16),
            pltpu.VMEM((D, KVD), BF16),
            pltpu.VMEM((ROWS, KVD, SMAX), BF16),
            pltpu.VMEM((ROWS, KVD, SMAX), BF16),
            pltpu.VMEM((STEPS, KVD, ROWS), BF16),
            pltpu.VMEM((STEPS, KVD, ROWS), BF16),
            pltpu.VMEM((ROWS * 8, 128), F32),
            pltpu.VMEM((ROWS * 8, 128), F32),
            pltpu.SemaphoreType.DMA((3,)),
            pltpu.SemaphoreType.DMA((STEPS,)),
            pltpu.SemaphoreType.DMA((STEPS,)),
            pltpu.SemaphoreType.DMA((2, STEPS)),
        ],
        input_output_aliases={10: 1, 11: 2} if outs else {},
        compiler_params=pltpu.CompilerParams(vmem_limit_bytes=50 * 2 ** 20),
        name=f"attn{layer}",
    )(seq_lens, hidden, cos, sin, g_attn, w_q, w_k, w_v, k_cache, v_cache, *outs)


def mlp_kernel(layer, attn_ref, h_ref, g_ref, wo_hbm, wg_hbm, wu_hbm, wd_hbm, out_ref,
               wo, wg, wu, wd, send1, recv1, pair, recv2, hbuf, act,
               wsem, s1_send, s1_recv, s2_send, s2_recv, s3_send, s3_recv):
    me = lax.axis_index("tp")
    core = lax.rem(me, 2)
    sibling = me + 1 - 2 * core
    peer = lax.rem(me + 2, 4)

    def load(kind, j):
        src = (wo_hbm, wg_hbm, wu_hbm, wd_hbm)[kind].at[layer, :, pl.ds(j * CW, CW)]
        return pltpu.make_async_copy(src, (wo, wg, wu, wd)[kind].at[j], wsem.at[kind, j])

    for j in range(NCH):
        load(0, j).start()
    for j in range(NCH):
        load(1, j).start()
        load(2, j).start()
    for j in range(NCH):
        load(3, j).start()

    barrier = pltpu.get_barrier_semaphore()
    for other in (sibling, peer):
        pl.semaphore_signal(barrier, inc=1, device_id={"tp": other}, device_id_type=MESH)

    def remote(src, dst, ss, rs, to):
        return pltpu.make_async_remote_copy(src_ref=src, dst_ref=dst, send_sem=ss, recv_sem=rs,
                                            device_id={"tp": to}, device_id_type=MESH)

    def cols(j):
        return pl.ds(pl.multiple_of(j * CW, CW), CW)

    def copy1(r, j):
        return remote(send1.at[r, j], recv1.at[r, j], s1_send.at[r, j], s1_recv.at[r, j], sibling)

    def copy2(r, j):
        return remote(pair.at[r, j], recv2.at[r, j], s2_send.at[r, j], s2_recv.at[r, j], peer)

    def copy3(r, j):
        mine = hbuf.at[r, core * 2 + j]
        return remote(mine, mine, s3_send.at[r, j], s3_recv.at[r, j], sibling)

    def copy3_in(r, j):
        theirs = hbuf.at[r, 2 - core * 2 + j]
        return remote(theirs, theirs, s3_send.at[r, j], s3_recv.at[r, j], sibling)

    def all_reduce(r, product, residual):
        for j in range(2):
            send1[r, j] = product(2 - core * 2 + j).astype(BF16)
            if r == 0 and j == 0:
                pl.semaphore_wait(barrier, 2)
            copy1(r, j).start()
        own = [product(core * 2 + j) for j in range(2)]
        for j in range(2):
            copy1(r, j).wait_recv()
            pair[r, j] = (own[j] + recv1[r, j].astype(F32)).astype(BF16)
            copy2(r, j).start()
        for j in range(2):
            copy2(r, j).wait_recv()
            total = pair[r, j].astype(F32) + recv2[r, j].astype(F32)
            hbuf[r, core * 2 + j] = (residual(core * 2 + j).astype(F32) + total).astype(BF16)
            copy3(r, j).start()
        for j in range(2):
            copy3_in(r, j).wait_recv()
        for j in range(2):
            copy1(r, j).wait_send()
            copy2(r, j).wait_send()
            copy3(r, j).wait_send()

    for j in range(NCH):
        load(0, j).wait()
    attn = attn_ref[...]
    all_reduce(0, lambda j: jnp.dot(attn, wo[j], preferred_element_type=F32), lambda j: h_ref[:, cols(j)])

    hidden = jnp.concatenate([hbuf[0, j] for j in range(NCH)], axis=1)
    normed = norm_rows(hidden.astype(F32), g_ref[layer:layer + 1, :])
    for j in range(NCH):
        load(1, j).wait()
        gate = jnp.dot(normed, wg[j], preferred_element_type=F32)
        load(2, j).wait()
        up = jnp.dot(normed, wu[j], preferred_element_type=F32)
        act[:, j * CW:(j + 1) * CW] = (gate * jax.nn.sigmoid(gate) * up).astype(BF16)
    for j in range(NCH):
        load(3, j).wait()
    all_reduce(1, lambda j: jnp.dot(act[...], wd[j], preferred_element_type=F32), lambda j: hbuf[0, j])
    for j in range(NCH):
        out_ref[:, j * CW:(j + 1) * CW] = hbuf[1, j]


def mlp_call(layer, attn, hidden, g_mlp, w_o, w_gate, w_up, w_down):
    chunk = pltpu.VMEM((2, 2, ROWS, CW), BF16)
    return pl.pallas_call(
        functools.partial(mlp_kernel, layer),
        out_shape=jax.ShapeDtypeStruct((ROWS, D), BF16),
        in_specs=[VMEM, VMEM, VMEM] + [ANY] * 4,
        out_specs=VMEM,
        scratch_shapes=[
            pltpu.VMEM((NCH, QD, CW), BF16),
            pltpu.VMEM((NCH, D, CW), BF16),
            pltpu.VMEM((NCH, D, CW), BF16),
            pltpu.VMEM((NCH, FF, CW), BF16),
            chunk, chunk, chunk, chunk,
            pltpu.VMEM((2, NCH, ROWS, CW), BF16),
            pltpu.VMEM((ROWS, FF), BF16),
            pltpu.SemaphoreType.DMA((4, NCH)),
        ] + [pltpu.SemaphoreType.DMA((2, 2))] * 6,
        compiler_params=pltpu.CompilerParams(vmem_limit_bytes=50 * 2 ** 20, collective_id=layer, has_side_effects=True),
        name=f"mlp{layer}",
    )(attn, hidden, g_mlp, w_o, w_gate, w_up, w_down)


def solution(mesh):
    cache_spec = P(None, "dp", None, "tp", None)
    col_spec = P(None, None, "tp")
    row_spec = P(None, "tp", None)
    in_specs = (P("dp", None), P("dp"), cache_spec, cache_spec, P(None, None), col_spec, col_spec, col_spec,
                row_spec, P(None, None), col_spec, col_spec, row_spec)
    out_specs = (P("dp", None), cache_spec, cache_spec)

    def local_step(hidden, seq_lens, k_cache, v_cache, g_attn, w_q, w_k, w_v, w_o, g_mlp, w_gate, w_up, w_down):
        layers = k_cache.shape[0]
        kt = k_cache.transpose(0, 1, 3, 4, 2).reshape(layers, ROWS, KVD, SMAX)
        vt = v_cache.transpose(0, 1, 3, 4, 2).reshape(layers, ROWS, KVD, SMAX)
        angle = seq_lens.astype(F32)[:, None] * rope_freqs(HEAD)[None, :]
        cos = jnp.tile(jnp.cos(angle), (1, 4))
        sin = jnp.sin(angle)
        sin = jnp.concatenate([-sin, sin, -sin, sin], axis=1)
        outs = ()
        for layer in range(layers):
            attn, *outs = attn_call(layer, seq_lens, hidden, cos, sin, g_attn, w_q, w_k, w_v, kt, vt, outs)
            hidden = mlp_call(layer, attn, hidden, g_mlp, w_o, w_gate, w_up, w_down)

        def back(cache):
            return cache.reshape(layers, ROWS, 2, HEAD, SMAX).transpose(0, 1, 4, 2, 3)

        return hidden, back(outs[0]), back(outs[1])

    return jax.shard_map(local_step, mesh=mesh, in_specs=in_specs, out_specs=out_specs, check_vma=False)
```

time: 223 us -> 106 us (0.48)
  Pallas kernels: 0 us -> 97.8 us
  waiting for transfers between devices: 93.1 us -> 0 us
  matrix products: 61.2 us -> 0 us
  other arithmetic: 35.9 us -> 1.11 us
  between operations: 14.2 us -> 0.77 us
  local copies, waits for them, and re-layouts: 17.5 us -> 5.83 us
    pallas_call x0 -> x4, Pallas kernels: none -> 97.8 us  [the longest x2 55.2 us: mlp_call(): pl.pallas_call(functools.partial(mlp_kernel, layer), out_shape=jax.ShapeD...]
    psum x4 -> x0, waiting for transfers between devices: 93.1 us -> none  [the longest x2 61.8 us: local_step(): hidden = add_residual(hidden, lax.psum(attn_part, 'tp'))]
    dot_general x16 -> x0, matrix products: 61.2 us -> none  [the longest x2 18.4 us: mlp_partial(): return jnp.dot(mlp_act, w_down, preferred_element_type=jnp.float32)]
    select_n x1 -> x0, other arithmetic: 23 us -> none  [write_cache(): return jnp.where(at_new, new_rows[:, :, None], cache)]
    dot_general x9 -> x0, local copies, waits for them, and re-layouts: 14.9 us -> none  [the longest x3 9.1 us: attention_block(): jnp.dot(normed, w_q, preferred_element_type=jnp.float32)]
    reduce_sum x6 -> x0, other arithmetic: 6.94 us -> none  [the longest x4 5.22 us: rms_norm(): jnp.mean(hidden_f * hidden_f, axis=-1, keepdims=True) + NORM_EPS]
    unnamed x12 -> x21, local copies, waits for them, and re-layouts: 0.03 us -> 5.66 us
    convert_element_type x5 -> x1, other arithmetic: 3.93 us -> 0.66 us  [local_step(): angle = seq_lens.astype(F32)[:, None] * rope_freqs(HEAD)[None, :]]
  transfers between devices with their start and end apart: 4 -> 0, of which waited for: 4 -> 0; matrix products, arithmetic and copies ran while one was open for 13% -> 0% of each run, Pallas kernels for 0% -> 0%
where the time goes in v1:
time: 106 us
  Pallas kernels  97.8 us (92%)
  local copies, waits for them, and re-layouts  5.83 us (6%)
  other arithmetic  1.11 us (1%)
    pallas_call x2, Pallas kernels, mlp_call(): pl.pallas_call(functools.partial(mlp_kernel, layer), out_shape=jax.ShapeD...  55.2 us
    pallas_call x2, Pallas kernels, attn_call(): pl.pallas_call(functools.partial(attn_kernel, layer, bool(outs)), out_sha...  42.6 us
    unnamed x21, local copies, waits for them, and re-layouts  5.66 us

profile of v1, /device:TPU:0, one launch (start us, length us, event | category | flops | bytes accessed | tf_op | source)
XLA Modules:
  0.0 105.5 jit_solution(16225704603866696446)
XLA Ops:
  0.6 0.7 convert_element_type.10
  1.3 0.3 fusion
  1.6 0.1 pad_maximum_fusion.refs_3_
  1.8 0.1 copy.22
  1.8 0.1 copy.23.refs_2_
  1.9 0.0 copy-start
  1.9 1.2 %copy-done = bf16[2,2048,128]{2,1,0:T(8,128)(2,1)S(1)} copy-done((bf16[2,2048,128]{2,1,0:T(8,128)(2,1)S(1)}, bf16[2,2048,128]{2,1,0:T(8,128)(2,1)}, u32[]{:S(2)}) %copy-start) | copy-done | bytes 1048600
  3.2 1.2 %copy-done.2 = bf16[2,2048,128]{2,1,0:T(8,128)(2,1)S(1)} copy-done((bf16[2,2048,128]{2,1,0:T(8,128)(2,1)S(1)}, bf16[2,2048,128]{2,1,0:T(8,128)(2,1)}, u32[]{:S(2)}) %copy-start.2) | copy-done | bytes 1048600
  4.4 1.0 copy-done.4
  5.4 0.7 copy-done.6
  6.1 0.7 copy-done.9
  6.8 21.3 %attn0.1 = (bf16[128,512]{1,0:T(8,128)(2,1)S(1)}, bf16[2,128,128,256]{3,2,1,0:T(8,128)(2,1)}, bf16[2,128,128,256]{3,2,1,0:T(8,128)(2,1)}) custom-call(s32[128]{0:T(128)S(1)} %copy-done.9, bf16[128,2048]{1,0:T(8,128)(2,1)S(1)} %copy-done.4, f32[128,128]{1,0:T(8,128)S(1)} %copy.23.refs_2_, f32[128,128]{1,0:T(8,128)S(1)} %pad_maximum_fusion.refs_3_, ...), custom_call_target="tpu_custom_call" | custom-call | tf_op jit(solution)/shard_map/attn0/pallas_call | solution.py:158
  28.1 0.0 copy-done.5
  28.1 0.0 copy-done.8
  28.1 0.0 copy-start.1
  28.1 0.0 copy-start.3
  28.1 0.0 copy-start.7
  28.2 27.8 %mlp0.1.refs_1_.h_ref = bf16[128,2048]{1,0:T(8,128)(2,1)S(1)} custom-call(bf16[128,512]{1,0:T(8,128)(2,1)S(1)} %get-tuple-element.9.attn_ref, bf16[128,2048]{1,0:T(8,128)(2,1)S(1)} %copy-done.5, bf16[2,2048]{1,0:T(2,128)(2,1)S(1)} %copy-done.8, bf16[2,512,2048]{2,1,0:T(8,128)(2,1)} %wo_hbm.3, bf16[2,2048,2048]{2,1,0:T(8,128)(2,1)} %wg_hbm.3, ...), custom_call_target="tpu_custom_call" | custom-call | tf_op jit(solution)/shard_map/mlp0/pallas_call | solution.py:274
  55.9 0.0 copy-done.1
  55.9 0.0 copy-done.3
  55.9 0.0 copy-done.7
  55.9 21.3 %attn1.1 = (bf16[128,512]{1,0:T(8,128)(2,1)S(1)}, bf16[2,128,128,256]{3,2,1,0:T(8,128)(2,1)}, bf16[2,128,128,256]{3,2,1,0:T(8,128)(2,1)}) custom-call(s32[128]{0:T(128)S(1)} %copy-done.9, bf16[128,2048]{1,0:T(8,128)(2,1)S(1)} %mlp0.1.refs_1_.h_ref, f32[128,128]{1,0:T(8,128)S(1)} %copy.23.refs_2_, ...), custom_call_target="tpu_custom_call", output_to_operand_aliasing={{1}: (10, {}), {2}: (11, {})} | custom-call | tf_op jit(solution)/shard_map/attn1/pallas_call | solution.py:158
  77.3 27.5 %mlp1.1 = bf16[128,2048]{1,0:T(8,128)(2,1)S(1)} custom-call(bf16[128,512]{1,0:T(8,128)(2,1)S(1)} %get-tuple-element.12.attn_ref, bf16[128,2048]{1,0:T(8,128)(2,1)S(1)} %mlp0.1.refs_1_.h_ref, bf16[2,2048]{1,0:T(2,128)(2,1)S(1)} %copy-done.8, bf16[2,512,2048]{2,1,0:T(8,128)(2,1)} %wo_hbm.3, bf16[2,2048,2048]{2,1,0:T(8,128)(2,1)} %wg_hbm.3, ...), custom_call_target="tpu_custom_call" | custom-call | tf_op jit(solution)/shard_map/mlp1/pallas_call | solution.py:274
  104.7 0.8 copy.28
  (8 shorter events, 0.0 us)
Async XLA Ops:
  1.9 1.2 %copy-start = (bf16[2,2048,128]{2,1,0:T(8,128)(2,1)S(1)}, bf16[2,2048,128]{2,1,0:T(8,128)(2,1)}, u32[]{:S(2)}) copy-start(bf16[2,2048,128]{2,1,0:T(8,128)(2,1)} %refs_6_.3) | copy-start | bytes 3145732
  3.2 1.2 %copy-start.2 = (bf16[2,2048,128]{2,1,0:T(8,128)(2,1)S(1)}, bf16[2,2048,128]{2,1,0:T(8,128)(2,1)}, u32[]{:S(2)}) copy-start(bf16[2,2048,128]{2,1,0:T(8,128)(2,1)} %refs_7_.3) | copy-start | bytes 3145732
  4.4 1.0 copy-start.4
  5.4 0.7 copy-start.6
  6.1 0.7 copy-start.9
  6.8 21.3 %copy-start.5 = (bf16[128,2048]{1,0:T(8,128)(2,1)S(1)}, bf16[128,2048]{1,0:T(8,128)(2,1)}, u32[]{:S(2)}) copy-start(bf16[128,2048]{1,0:T(8,128)(2,1)} %h_ref.1) | copy-start | bytes 1572868
  6.8 21.3 %copy-start.8 = (bf16[2,2048]{1,0:T(2,128)(2,1)S(1)}, bf16[2,2048]{1,0:T(2,128)(2,1)}, u32[]{:S(2)}) copy-start(bf16[2,2048]{1,0:T(2,128)(2,1)} %g_ref.3) | copy-start | bytes 24580
  28.1 27.8 %copy-start.1 = (bf16[2,2048,128]{2,1,0:T(8,128)(2,1)S(1)}, bf16[2,2048,128]{2,1,0:T(8,128)(2,1)}, u32[]{:S(2)}) copy-start(bf16[2,2048,128]{2,1,0:T(8,128)(2,1)} %refs_6_.3) | copy-start | bytes 3145732
  28.1 27.8 %copy-start.3 = (bf16[2,2048,128]{2,1,0:T(8,128)(2,1)S(1)}, bf16[2,2048,128]{2,1,0:T(8,128)(2,1)}, u32[]{:S(2)}) copy-start(bf16[2,2048,128]{2,1,0:T(8,128)(2,1)} %refs_7_.3) | copy-start | bytes 3145732
  28.1 27.8 %copy-start.7 = (bf16[2,2048]{1,0:T(2,128)(2,1)S(1)}, bf16[2,2048]{1,0:T(2,128)(2,1)}, u32[]{:S(2)}) copy-start(bf16[2,2048]{1,0:T(2,128)(2,1)} %refs_4_.3) | copy-start | bytes 24580

commit v2 on v1

--- a/solution.py
+++ b/solution.py
@@ -2,6 +2,7 @@
 
 import jax
 import jax.numpy as jnp
+import numpy as np
 from jax import lax
 from jax.experimental import pallas as pl
 from jax.experimental.pallas import tpu as pltpu
@@ -21,26 +22,25 @@
 KVD = 128
 QD = 512
 FF = 2048
-SEQS = 8
+SEQS = 16
 STEPS = ROWS // SEQS
 CW = 512
 NCH = D // CW
 F32 = jnp.float32
 BF16 = jnp.bfloat16
 MESH = pl.DeviceIdType.MESH
-ANY = pl.BlockSpec(memory_space=pl.ANY)
 VMEM = pl.BlockSpec(memory_space=pltpu.VMEM)
-SMEM = pl.BlockSpec(memory_space=pltpu.SMEM)
+HBM = pl.BlockSpec(memory_space=pltpu.HBM)
 
 
 def rope_freqs(head_dim):
-    freq_expo = jnp.arange(0, head_dim, 2).astype(F32) / head_dim
-    inv_freq = 1.0 / (ROPE_THETA ** freq_expo)
-    wavelen = 2.0 * jnp.pi / inv_freq
+    freq_expo = np.arange(0, head_dim, 2).astype(np.float32) / np.float32(head_dim)
+    inv_freq = 1.0 / (ROPE_THETA ** freq_expo.astype(np.float64))
+    wavelen = 2.0 * np.pi / inv_freq
     smooth = (ORIG_CONTEXT / wavelen - LOW_FACTOR) / (HIGH_FACTOR - LOW_FACTOR)
     blended = (1.0 - smooth) * inv_freq / ROPE_FACTOR + smooth * inv_freq
-    return jnp.where(wavelen > ORIG_CONTEXT / LOW_FACTOR, inv_freq / ROPE_FACTOR,
-                     jnp.where(wavelen < ORIG_CONTEXT / HIGH_FACTOR, inv_freq, blended))
+    return np.where(wavelen > ORIG_CONTEXT / LOW_FACTOR, inv_freq / ROPE_FACTOR,
+                    np.where(wavelen < ORIG_CONTEXT / HIGH_FACTOR, inv_freq, blended)).astype(np.float32)
 
 
 def norm_rows(hidden_f, gain):
@@ -55,16 +55,14 @@
 
 
 def attn_kernel(layer, aliased, *refs):
-    if aliased:
-        (seq_ref, h_ref, cos_ref, sin_ref, g_ref, wq_hbm, wk_hbm, wv_hbm, k_hbm, v_hbm, _, _,
-         out_ref, ko_hbm, vo_hbm, wq, wk, wv, kbuf, vbuf, knew, vnew, qrow, orow, wsem, ksem, vsem, osem) = refs
-    else:
-        (seq_ref, h_ref, cos_ref, sin_ref, g_ref, wq_hbm, wk_hbm, wv_hbm, k_hbm, v_hbm,
-         out_ref, ko_hbm, vo_hbm, wq, wk, wv, kbuf, vbuf, knew, vnew, qrow, orow, wsem, ksem, vsem, osem) = refs
-
-    def load_w(i):
-        src, dst = ((wk_hbm, wk), (wv_hbm, wv), (wq_hbm, wq))[i]
-        return pltpu.make_async_copy(src.at[layer], dst, wsem.at[i])
+    seq_hbm, seqv_hbm, freq_hbm, h_hbm, g_hbm, wq_hbm, wk_hbm, wv_hbm, k_hbm, v_hbm = refs[:10]
+    (out_ref, ko_hbm, vo_hbm, seq_ref, seqv, freq, h_ref, g_ref, wq, wk, wv, kbuf, vbuf, knew, vnew, qrow, orow,
+     sem, ksem, vsem, osem) = refs[12 if aliased else 10:]
+
+    def small(i):
+        src, dst = ((seqv_hbm, seqv), (freq_hbm, freq), (h_hbm, h_ref), (g_hbm, g_ref), (wk_hbm.at[layer], wk),
+                    (wv_hbm.at[layer], wv), (wq_hbm.at[layer], wq), (seq_hbm, seq_ref))[i]
+        return pltpu.make_async_copy(src, dst, sem.at[i])
 
     def load_k(i):
         return pltpu.make_async_copy(k_hbm.at[layer, pl.ds(i * SEQS, SEQS)], kbuf.at[pl.ds(i * SEQS, SEQS)], ksem.at[i])
@@ -78,25 +76,29 @@
     def store_v(i):
         return pltpu.make_async_copy(vbuf.at[pl.ds(i * SEQS, SEQS)], vo_hbm.at[layer, pl.ds(i * SEQS, SEQS)], osem.at[1, i])
 
-    for i in range(3):
-        load_w(i).start()
-    for i in range(STEPS):
+    for i in range(8):
+        small(i).start()
+    load_k(0).start()
+    load_v(0).start()
+
+    small(0).wait()
+    small(1).wait()
+    angle = jnp.broadcast_to(seqv[...].astype(F32), (ROWS, 128)).T * freq[...]
+    cos = jnp.cos(angle)
+    sin = jnp.sin(angle)
+    lane = lax.broadcasted_iota(jnp.int32, (ROWS, 128), 1)
+    sin = jnp.where(lane % HEAD < HEAD // 2, -sin, sin)
+    small(2).wait()
+    small(3).wait()
+    normed = norm_rows(h_ref[...].astype(F32), g_ref[layer:layer + 1, :])
+    small(4).wait()
+    small(5).wait()
+    small(6).wait()
+    for i in range(1, STEPS):
         load_k(i).start()
         load_v(i).start()
-
-    normed = norm_rows(h_ref[...].astype(F32), g_ref[layer:layer + 1, :])
-    cos = cos_ref[...]
-    sin = sin_ref[...]
-    load_w(0).wait()
-    k_rot = rope_slab(jnp.dot(normed, wk[...], preferred_element_type=F32), cos, sin).astype(BF16).astype(F32).T
-    load_w(1).wait()
-    v_row = jnp.dot(normed, wv[...], preferred_element_type=F32).astype(BF16).astype(F32).T
-    for i in range(STEPS):
-        shift = (ROWS - i * SEQS) % ROWS
-        knew[i] = (pltpu.roll(k_rot, shift, 1) if shift else k_rot).astype(BF16)
-        vnew[i] = (pltpu.roll(v_row, shift, 1) if shift else v_row).astype(BF16)
-    load_w(2).wait()
-    lane = lax.broadcasted_iota(jnp.int32, (ROWS, 128), 1)
+    knew[...] = rope_slab(jnp.dot(normed, wk[...], preferred_element_type=F32), cos, sin).astype(BF16).astype(F32).T
+    vnew[...] = jnp.dot(normed, wv[...], preferred_element_type=F32).astype(BF16).astype(F32).T
     for slab_idx in range(4):
         slab = jnp.dot(normed, wq[:, slab_idx * 128:(slab_idx + 1) * 128], preferred_element_type=F32)
         slab = rope_slab(slab, cos, sin).astype(BF16).astype(F32)
@@ -105,6 +107,7 @@
             hg = slab_idx * 2 + half
             kv = hg // 4
             qrow[pl.ds(hg, ROWS, stride=8), :] = jnp.where(lane // HEAD == kv, slab if kv == half else turned, 0.0)
+    small(7).wait()
 
     def step(i, carry):
         load_k(i).wait()
@@ -114,12 +117,19 @@
         row16 = lax.broadcasted_iota(jnp.int32, (16, 128), 0)
         row8 = lax.broadcasted_iota(jnp.int32, (8, 128), 0)
         lane_o = lax.broadcasted_iota(jnp.int32, (8, 128), 1)
-        for j in range(SEQS):
-            b = i * SEQS + j
-            here = lane16 == seq_ref[b].astype(jnp.int16)
-            kbuf[b] = jnp.where(here, jnp.broadcast_to(knew[i, :, j:j + 1], (KVD, SMAX)), kbuf[b])
-            vbuf[b] = jnp.where(here, jnp.broadcast_to(vnew[i, :, j:j + 1], (KVD, SMAX)), vbuf[b])
+        shift = lax.rem(ROWS - i * SEQS, ROWS)
+
+        def insert(buf, new_ref):
+            new = pltpu.roll(new_ref[...], shift, 1)
+            for j in range(SEQS):
+                b = i * SEQS + j
+                column = jnp.broadcast_to(new[:, j:j + 1], (KVD, 128)).astype(BF16)
+                here = lane16 == seq_ref[0, b].astype(jnp.int16)
+                buf[b] = jnp.where(here, jnp.concatenate([column, column], axis=1), buf[b])
+
+        insert(kbuf, knew)
         store_k(i).start()
+        insert(vbuf, vnew)
         store_v(i).start()
         scores = []
         for p in range(SEQS // 2):
@@ -132,7 +142,7 @@
             b = i * SEQS + 2 * p
             halves = []
             for j in range(2):
-                s = jnp.where(lane8 <= seq_ref[b + j], scores[p][8 * j:8 * j + 8], -1e30)
+                s = jnp.where(lane8 <= seq_ref[0, b + j], scores[p][8 * j:8 * j + 8], -1e30)
                 e = jnp.exp(s - jnp.max(s, axis=-1, keepdims=True))
                 halves.append(e / jnp.sum(e, axis=-1, keepdims=True))
             prob = jnp.concatenate(halves, axis=0).astype(BF16)
@@ -153,24 +163,29 @@
         store_v(i).wait()
 
 
-def attn_call(layer, seq_lens, hidden, cos, sin, g_attn, w_q, w_k, w_v, k_cache, v_cache, outs=()):
+def attn_call(layer, seq_lens, freq, hidden, g_attn, w_q, w_k, w_v, k_cache, v_cache, outs=()):
     cache = jax.ShapeDtypeStruct(k_cache.shape, BF16)
     return pl.pallas_call(
         functools.partial(attn_kernel, layer, bool(outs)),
         out_shape=(jax.ShapeDtypeStruct((ROWS, QD), BF16), cache, cache),
-        in_specs=[SMEM, VMEM, VMEM, VMEM, VMEM] + [ANY] * (5 + len(outs)),
-        out_specs=(VMEM, ANY, ANY),
+        in_specs=[HBM] * (10 + len(outs)),
+        out_specs=(VMEM, HBM, HBM),
         scratch_shapes=[
+            pltpu.SMEM((1, ROWS), jnp.int32),
+            pltpu.VMEM((1, ROWS), jnp.int32),
+            pltpu.VMEM((1, 128), F32),
+            pltpu.VMEM((ROWS, D), BF16),
+            pltpu.VMEM(g_attn.shape, BF16),
             pltpu.VMEM((D, QD), BF16),
             pltpu.VMEM((D, KVD), BF16),
             pltpu.VMEM((D, KVD), BF16),
             pltpu.VMEM((ROWS, KVD, SMAX), BF16),
             pltpu.VMEM((ROWS, KVD, SMAX), BF16),
-            pltpu.VMEM((STEPS, KVD, ROWS), BF16),
-            pltpu.VMEM((STEPS, KVD, ROWS), BF16),
+            pltpu.VMEM((KVD, ROWS), F32),
+            pltpu.VMEM((KVD, ROWS), F32),
             pltpu.VMEM((ROWS * 8, 128), F32),
             pltpu.VMEM((ROWS * 8, 128), F32),
-            pltpu.SemaphoreType.DMA((3,)),
+            pltpu.SemaphoreType.DMA((8,)),
             pltpu.SemaphoreType.DMA((STEPS,)),
             pltpu.SemaphoreType.DMA((STEPS,)),
             pltpu.SemaphoreType.DMA((2, STEPS)),
@@ -178,12 +193,12 @@
         input_output_aliases={10: 1, 11: 2} if outs else {},
         compiler_params=pltpu.CompilerParams(vmem_limit_bytes=50 * 2 ** 20),
         name=f"attn{layer}",
-    )(seq_lens, hidden, cos, sin, g_attn, w_q, w_k, w_v, k_cache, v_cache, *outs)
-
-
-def mlp_kernel(layer, attn_ref, h_ref, g_ref, wo_hbm, wg_hbm, wu_hbm, wd_hbm, out_ref,
-               wo, wg, wu, wd, send1, recv1, pair, recv2, hbuf, act,
-               wsem, s1_send, s1_recv, s2_send, s2_recv, s3_send, s3_recv):
+    )(seq_lens, seq_lens, freq, hidden, g_attn, w_q, w_k, w_v, k_cache, v_cache, *outs)
+
+
+def mlp_kernel(layer, attn_ref, h_hbm, g_hbm, wo_hbm, wg_hbm, wu_hbm, wd_hbm, out_ref,
+               h_ref, g_ref, wo, wg, wu, wd, send1, recv1, pair, recv2, hbuf, act,
+               hsem, wsem, s1_send, s1_recv, s2_send, s2_recv, s3_send, s3_recv):
     me = lax.axis_index("tp")
     core = lax.rem(me, 2)
     sibling = me + 1 - 2 * core
@@ -195,11 +210,10 @@
 
     for j in range(NCH):
         load(0, j).start()
-    for j in range(NCH):
-        load(1, j).start()
-        load(2, j).start()
-    for j in range(NCH):
-        load(3, j).start()
+    load_h = pltpu.make_async_copy(h_hbm, h_ref, hsem.at[0])
+    load_g = pltpu.make_async_copy(g_hbm, g_ref, hsem.at[1])
+    load_h.start()
+    load_g.start()
 
     barrier = pltpu.get_barrier_semaphore()
     for other in (sibling, peer):
@@ -227,16 +241,20 @@
         return remote(theirs, theirs, s3_send.at[r, j], s3_recv.at[r, j], sibling)
 
     def all_reduce(r, product, residual):
-        for j in range(2):
+        def to_sibling(j):
             send1[r, j] = product(2 - core * 2 + j).astype(BF16)
-            if r == 0 and j == 0:
-                pl.semaphore_wait(barrier, 2)
             copy1(r, j).start()
-        own = [product(core * 2 + j) for j in range(2)]
-        for j in range(2):
+
+        def to_peer(j, own):
             copy1(r, j).wait_recv()
-            pair[r, j] = (own[j] + recv1[r, j].astype(F32)).astype(BF16)
+            pair[r, j] = (own + recv1[r, j].astype(F32)).astype(BF16)
             copy2(r, j).start()
+
+        to_sibling(0)
+        own0 = product(core * 2)
+        to_sibling(1)
+        to_peer(0, own0)
+        to_peer(1, product(core * 2 + 1))
         for j in range(2):
             copy2(r, j).wait_recv()
             total = pair[r, j].astype(F32) + recv2[r, j].astype(F32)
@@ -251,7 +269,15 @@
 
     for j in range(NCH):
         load(0, j).wait()
+    for j in range(NCH):
+        load(1, j).start()
+        load(2, j).start()
+    for j in range(NCH):
+        load(3, j).start()
+    load_h.wait()
+    load_g.wait()
     attn = attn_ref[...]
+    pl.semaphore_wait(barrier, 2)
     all_reduce(0, lambda j: jnp.dot(attn, wo[j], preferred_element_type=F32), lambda j: h_ref[:, cols(j)])
 
     hidden = jnp.concatenate([hbuf[0, j] for j in range(NCH)], axis=1)
@@ -274,9 +300,11 @@
     return pl.pallas_call(
         functools.partial(mlp_kernel, layer),
         out_shape=jax.ShapeDtypeStruct((ROWS, D), BF16),
-        in_specs=[VMEM, VMEM, VMEM] + [ANY] * 4,
+        in_specs=[VMEM] + [HBM] * 6,
         out_specs=VMEM,
         scratch_shapes=[
+            pltpu.VMEM((ROWS, D), BF16),
+            pltpu.VMEM(g_mlp.shape, BF16),
             pltpu.VMEM((NCH, QD, CW), BF16),
             pltpu.VMEM((NCH, D, CW), BF16),
             pltpu.VMEM((NCH, D, CW), BF16),
@@ -284,6 +312,7 @@
             chunk, chunk, chunk, chunk,
             pltpu.VMEM((2, NCH, ROWS, CW), BF16),
             pltpu.VMEM((ROWS, FF), BF16),
+            pltpu.SemaphoreType.DMA((2,)),
             pltpu.SemaphoreType.DMA((4, NCH)),
         ] + [pltpu.SemaphoreType.DMA((2, 2))] * 6,
         compiler_params=pltpu.CompilerParams(vmem_limit_bytes=50 * 2 ** 20, collective_id=layer, has_side_effects=True),
@@ -303,13 +332,14 @@
         layers = k_cache.shape[0]
         kt = k_cache.transpose(0, 1, 3, 4, 2).reshape(layers, ROWS, KVD, SMAX)
         vt = v_cache.transpose(0, 1, 3, 4, 2).reshape(layers, ROWS, KVD, SMAX)
-        angle = seq_lens.astype(F32)[:, None] * rope_freqs(HEAD)[None, :]
-        cos = jnp.tile(jnp.cos(angle), (1, 4))
-        sin = jnp.sin(angle)
-        sin = jnp.concatenate([-sin, sin, -sin, sin], axis=1)
+        freq = jnp.asarray(np.tile(rope_freqs(HEAD), 4)[None, :])
+        seq_row = seq_lens.reshape(1, ROWS)
+        hidden, g_attn, w_q, w_k, w_v, w_o, g_mlp, w_gate, w_up, w_down, kt, vt, freq, seq_row = (
+            pltpu.with_memory_space_constraint(x, pltpu.HBM)
+            for x in (hidden, g_attn, w_q, w_k, w_v, w_o, g_mlp, w_gate, w_up, w_down, kt, vt, freq, seq_row))
         outs = ()
         for layer in range(layers):
-            attn, *outs = attn_call(layer, seq_lens, hidden, cos, sin, g_attn, w_q, w_k, w_v, kt, vt, outs)
+            attn, *outs = attn_call(layer, seq_row, freq, hidden, g_attn, w_q, w_k, w_v, kt, vt, outs)
             hidden = mlp_call(layer, attn, hidden, g_mlp, w_o, w_gate, w_up, w_down)
 
         def back(cache):

time: 106 us -> 86.9 us (0.82)
  Pallas kernels: 97.8 us -> 85.3 us
  local copies, waits for them, and re-layouts: 5.83 us -> 0.8 us
  other arithmetic: 1.11 us -> 0 us
    pallas_call x2, Pallas kernels: 42.6 us -> 29.5 us  [attn_call(): pl.pallas_call(functools.partial(attn_kernel, layer, bool(outs)), out_sha...]
    unnamed x21 -> x1, local copies, waits for them, and re-layouts: 5.66 us -> 0.8 us
where the time goes in v2:
time: 86.9 us; the launch traced here: 86.8 us
  Pallas kernels  85.3 us (98%)
    pallas_call x2, Pallas kernels, mlp_call(): pl.pallas_call(functools.partial(mlp_kernel, layer), out_shape=jax.ShapeD...  55.8 us
    pallas_call x2, Pallas kernels, attn_call(): pl.pallas_call(functools.partial(attn_kernel, layer, bool(outs)), out_sha...  29.5 us

profile of v2, /device:TPU:0, one launch (start us, length us, event | category | flops | bytes accessed | tf_op | source)
XLA Modules:
  0.0 86.8 jit_solution(5507035397756205766)
XLA Ops:
  0.6 14.8 %attn0.1 = (bf16[128,512]{1,0:T(8,128)(2,1)S(1)}, bf16[2,128,128,256]{3,2,1,0:T(8,128)(2,1)}, bf16[2,128,128,256]{3,2,1,0:T(8,128)(2,1)}) custom-call(s32[1,128]{1,0:T(1,128)} %bitcast.19, s32[1,128]{1,0:T(1,128)} %bitcast.20, f32[1,128]{1,0:T(1,128)} %constant.2.clone.refs_2_, bf16[128,2048]{1,0:T(8,128)(2,1)} %h_hbm.1, bf16[2,2048]{1,0:T(2,128)(2,1)} %refs_4_.3, ...), custom_call_target="tpu_custom_call" | custom-call | tf_op jit(solution)/shard_map/attn0/pallas_call | solution.py:168
  15.5 28.0 %mlp0.1.refs_3_.h_hbm = bf16[128,2048]{1,0:T(8,128)(2,1)S(1)} custom-call(bf16[128,512]{1,0:T(8,128)(2,1)S(1)} %get-tuple-element.9.attn_ref, bf16[128,2048]{1,0:T(8,128)(2,1)} %h_hbm.1, bf16[2,2048]{1,0:T(2,128)(2,1)} %g_hbm.3, bf16[2,512,2048]{2,1,0:T(8,128)(2,1)} %wo_hbm.3, bf16[2,2048,2048]{2,1,0:T(8,128)(2,1)} %wg_hbm.3, bf16[2,2048,2048]{2,1,0:T(8,128)(2,1)} %wu_hbm.3, ...), custom_call_target="tpu_custom_call" | custom-call | tf_op jit(solution)/shard_map/mlp0/pallas_call | solution.py:300
  43.5 14.7 %attn1.1 = (bf16[128,512]{1,0:T(8,128)(2,1)S(1)}, bf16[2,128,128,256]{3,2,1,0:T(8,128)(2,1)}, bf16[2,128,128,256]{3,2,1,0:T(8,128)(2,1)}) custom-call(s32[1,128]{1,0:T(1,128)} %bitcast.21, s32[1,128]{1,0:T(1,128)} %bitcast.22, f32[1,128]{1,0:T(1,128)} %constant.2.clone.refs_2_, ...), custom_call_target="tpu_custom_call", output_to_operand_aliasing={{1}: (10, {}), {2}: (11, {})} | custom-call | tf_op jit(solution)/shard_map/attn1/pallas_call | solution.py:168
  58.2 27.7 %mlp1.1 = bf16[128,2048]{1,0:T(8,128)(2,1)S(1)} custom-call(bf16[128,512]{1,0:T(8,128)(2,1)S(1)} %get-tuple-element.12.attn_ref, bf16[128,2048]{1,0:T(8,128)(2,1)S(1)} %mlp0.1.refs_3_.h_hbm, bf16[2,2048]{1,0:T(2,128)(2,1)} %g_hbm.3, bf16[2,512,2048]{2,1,0:T(8,128)(2,1)} %wo_hbm.3, bf16[2,2048,2048]{2,1,0:T(8,128)(2,1)} %wg_hbm.3, ...), custom_call_target="tpu_custom_call" | custom-call | tf_op jit(solution)/shard_map/mlp1/pallas_call | solution.py:300
  86.0 0.8 copy.22

commit v3 on v2

v3 whole, which is shorter than its diff:
```python
import functools

import jax
import jax.numpy as jnp
import numpy as np
from jax import lax
from jax.experimental import pallas as pl
from jax.experimental.pallas import tpu as pltpu
from jax.sharding import PartitionSpec as P

NORM_EPS = 1e-5
ROPE_THETA = 500000.0
ROPE_FACTOR = 8.0
LOW_FACTOR = 1.0
HIGH_FACTOR = 4.0
ORIG_CONTEXT = 8192.0

ROWS = 128
D = 2048
SMAX = 256
HEAD = 64
KVD = 128
QD = 512
FF = 2048
SEQS = 16
STEPS = ROWS // SEQS
CW = 512
NCH = D // CW
HALF = D // 2
RC = 32
NRC = ROWS // RC
F32 = jnp.float32
BF16 = jnp.bfloat16
MESH = pl.DeviceIdType.MESH
VMEM = pl.BlockSpec(memory_space=pltpu.VMEM)
HBM = pl.BlockSpec(memory_space=pltpu.HBM)


def rope_freqs(head_dim):
    freq_expo = np.arange(0, head_dim, 2).astype(np.float32) / np.float32(head_dim)
    inv_freq = 1.0 / (ROPE_THETA ** freq_expo.astype(np.float64))
    wavelen = 2.0 * np.pi / inv_freq
    smooth = (ORIG_CONTEXT / wavelen - LOW_FACTOR) / (HIGH_FACTOR - LOW_FACTOR)
    blended = (1.0 - smooth) * inv_freq / ROPE_FACTOR + smooth * inv_freq
    return np.where(wavelen > ORIG_CONTEXT / LOW_FACTOR, inv_freq / ROPE_FACTOR,
                    np.where(wavelen < ORIG_CONTEXT / HIGH_FACTOR, inv_freq, blended)).astype(np.float32)


def norm_rows(hidden_f, gain):
    inv_rms = lax.rsqrt(jnp.mean(hidden_f * hidden_f, axis=-1, keepdims=True) + NORM_EPS)
    return (hidden_f * inv_rms * gain.astype(F32)).astype(BF16)


def rope_slab(slab, cos, sin):
    lane = lax.broadcasted_iota(jnp.int32, slab.shape, 1)
    other = jnp.where(lane % HEAD < HEAD // 2, pltpu.roll(slab, 128 - HEAD // 2, 1), pltpu.roll(slab, HEAD // 2, 1))
    return slab * cos + other * sin


def layer_kernel(layer, seq_hbm, seqv_hbm, freq_hbm, h_hbm, ga_hbm, gm_hbm, wq_hbm, wk_hbm, wv_hbm, wo_hbm, wg_hbm, wu_hbm,
                 wd_hbm, k_hbm, v_hbm, out_ref, kbuf, vbuf, seq_ref, seqv, freq, h_ref, ga, gm, wq, wk, wv, wo, wg, wu, wd,
                 knew, vnew, qrow, orow, own1, send1, recv1, pair1, peer1, mid, send2, recv2, pair2, peer2, last, act,
                 sem, ksem, vsem, osem, wsem, sems1, sems2):
    me = lax.axis_index("tp")
    core = lax.rem(me, 2)
    sibling = me + 1 - 2 * core
    peer = lax.rem(me + 2, 4)

    barrier = pltpu.get_barrier_semaphore()
    for other in (sibling, peer):
        pl.semaphore_signal(barrier, inc=1, device_id={"tp": other}, device_id_type=MESH)

    def small(i):
        src, dst = ((seqv_hbm, seqv), (freq_hbm, freq), (h_hbm, h_ref), (ga_hbm, ga), (wk_hbm.at[layer], wk),
                    (wv_hbm.at[layer], wv), (wq_hbm.at[layer], wq), (seq_hbm, seq_ref), (gm_hbm, gm))[i]
        return pltpu.make_async_copy(src, dst, sem.at[i])

    def load_k(i):
        return pltpu.make_async_copy(k_hbm.at[layer, pl.ds(i * SEQS, SEQS)], kbuf.at[pl.ds(i * SEQS, SEQS)], ksem.at[i])

    def load_v(i):
        return pltpu.make_async_copy(v_hbm.at[layer, pl.ds(i * SEQS, SEQS)], vbuf.at[pl.ds(i * SEQS, SEQS)], vsem.at[i])

    def load_o(j):
        return pltpu.make_async_copy(wo_hbm.at[layer, :, pl.ds(j * HALF, HALF)], wo.at[j], osem.at[j])

    def load(kind, j):
        src = (wg_hbm, wu_hbm, wd_hbm)[kind].at[layer, :, pl.ds(j * CW, CW)]
        return pltpu.make_async_copy(src, (wg, wu, wd)[kind].at[j], wsem.at[kind, j])

    def remote(src, dst, sems, i, j, to):
        return pltpu.make_async_remote_copy(src_ref=src, dst_ref=dst, send_sem=sems.at[2 * i, j], recv_sem=sems.at[2 * i + 1, j],
                                            device_id={"tp": to}, device_id_type=MESH)

    for i in range(9):
        small(i).start()
    load_k(0).start()
    load_v(0).start()

    small(0).wait()
    small(1).wait()
    angle = jnp.broadcast_to(seqv[...].astype(F32), (ROWS, 128)).T * freq[...]
    cos = jnp.cos(angle)
    sin = jnp.sin(angle)
    lane = lax.broadcasted_iota(jnp.int32, (ROWS, 128), 1)
    sin = jnp.where(lane % HEAD < HEAD // 2, -sin, sin)
    small(2).wait()
    small(3).wait()
    normed = norm_rows(h_ref[...].astype(F32), ga[layer:layer + 1, :])
    small(4).wait()
    small(5).wait()
    small(6).wait()
    for i in range(1, STEPS):
        load_k(i).start()
        load_v(i).start()
        if i == 2:
            load_o(0).start()
            load_o(1).start()
    knew[...] = rope_slab(jnp.dot(normed, wk[...], preferred_element_type=F32), cos, sin).astype(BF16).astype(F32).T
    vnew[...] = jnp.dot(normed, wv[...], preferred_element_type=F32).astype(BF16).astype(F32).T
    for slab_idx in range(4):
        slab = jnp.dot(normed, wq[:, slab_idx * 128:(slab_idx + 1) * 128], preferred_element_type=F32)
        slab = rope_slab(slab, cos, sin).astype(BF16).astype(F32)
        turned = pltpu.roll(slab, HEAD, 1)
        for half in range(2):
            hg = slab_idx * 2 + half
            kv = hg // 4
            qrow[pl.ds(hg, ROWS, stride=8), :] = jnp.where(lane // HEAD == kv, slab if kv == half else turned, 0.0)
    small(7).wait()
    small(8).wait()
    pl.semaphore_wait(barrier, 2)

    def attend(i):
        load_k(i).wait()
        load_v(i).wait()
        lane16 = lax.broadcasted_iota(jnp.int16, (KVD, SMAX), 1)
        lane8 = lax.broadcasted_iota(jnp.int32, (8, SMAX), 1)
        row16 = lax.broadcasted_iota(jnp.int32, (16, 128), 0)
        row8 = lax.broadcasted_iota(jnp.int32, (8, 128), 0)
        lane_o = lax.broadcasted_iota(jnp.int32, (8, 128), 1)
        shift = lax.rem(ROWS - i * SEQS, ROWS)

        def insert(buf, new_ref):
            new = pltpu.roll(new_ref[...], shift, 1)
            for j in range(SEQS):
                b = i * SEQS + j
                column = jnp.broadcast_to(new[:, j:j + 1], (KVD, 128)).astype(BF16)
                here = lane16 == seq_ref[0, b].astype(jnp.int16)
                buf[b] = jnp.where(here, jnp.concatenate([column, column], axis=1), buf[b])

        insert(kbuf, knew)
        insert(vbuf, vnew)
        scores = []
        for p in range(SEQS // 2):
            b = i * SEQS + 2 * p
            q2 = qrow[pl.ds(b * 8, 16), :]
            qb = jnp.concatenate([jnp.where(row16 < 8, q2, 0.0), jnp.where(row16 >= 8, q2, 0.0)], axis=1).astype(BF16)
            kk = kbuf[pl.ds(b, 2)].reshape(2 * KVD, SMAX)
            scores.append(jnp.dot(qb, kk, preferred_element_type=F32) * (HEAD ** -0.5))
        for p in range(SEQS // 2):
            b = i * SEQS + 2 * p
            halves = []
            for j in range(2):
                s = jnp.where(lane8 <= seq_ref[0, b + j], scores[p][8 * j:8 * j + 8], -1e30)
                e = jnp.exp(s - jnp.max(s, axis=-1, keepdims=True))
                halves.append(e / jnp.sum(e, axis=-1, keepdims=True))
            prob = jnp.concatenate(halves, axis=0).astype(BF16)
            vv = vbuf[pl.ds(b, 2)].reshape(2 * KVD, SMAX)
            mix = lax.dot_general(prob, vv, (((1,), (1,)), ((), ())), preferred_element_type=F32)
            for j in range(2):
                m = mix[8 * j:8 * j + 8, 128 * j:128 * j + 128]
                orow[pl.ds((b + j) * 8, 8), :] = jnp.where((row8 < 4) == (lane_o < HEAD), m, pltpu.roll(m, HEAD, 1))

    def rows(rc):
        return pl.ds(pl.multiple_of(rc * RC, RC), RC)

    def copy1(rc):
        return remote(send1.at[rc], recv1.at[rc], sems1, 0, rc, sibling)

    def copy1_peer(rc):
        return remote(pair1.at[rc], peer1.at[rc], sems1, 1, rc, peer)

    def copy1_out(rc, half):
        return remote(mid.at[half, rows(rc)], mid.at[half, rows(rc)], sems1, 2, rc, sibling)

    def to_peer1(rc):
        copy1(rc).wait_recv()
        pair1[rc] = (own1[rc] + recv1[rc].astype(F32)).astype(BF16)
        copy1_peer(rc).start()

    def row_chunk(rc, carry):
        def step(i, c):
            attend(rc * (RC // SEQS) + i)
            return c

        lax.fori_loop(0, RC // SEQS, step, 0)
        parts = []
        lane_r = lax.broadcasted_iota(jnp.int32, (RC, 128), 1)
        for slab_idx in range(4):
            lower = orow[pl.ds(rc * RC * 8 + slab_idx * 2, RC, stride=8), :]
            upper = orow[pl.ds(rc * RC * 8 + slab_idx * 2 + 1, RC, stride=8), :]
            parts.append(jnp.where(lane_r < HEAD, lower, upper).astype(BF16))
        attn = jnp.concatenate(parts, axis=1)

        @pl.when(rc == 0)
        def _():
            load_o(0).wait()
            load_o(1).wait()

        send1[rc] = jnp.dot(attn, wo[1 - core], preferred_element_type=F32).astype(BF16)
        copy1(rc).start()
        own1[rc] = jnp.dot(attn, wo[core], preferred_element_type=F32)

        @pl.when(rc > 0)
        def _():
            to_peer1(rc - 1)

        @pl.when(rc == 1)
        def _():
            for j in range(NCH):
                load(0, j).start()
                load(1, j).start()

        @pl.when(rc == 2)
        def _():
            for j in range(NCH):
                load(2, j).start()

        return carry

    lax.fori_loop(0, NRC, row_chunk, 0)
    to_peer1(NRC - 1)
    for rc in range(NRC):
        copy1_peer(rc).wait_recv()
        total = pair1[rc].astype(F32) + peer1[rc].astype(F32)
        residual = h_ref[rc * RC:(rc + 1) * RC, pl.ds(pl.multiple_of(core * HALF, HALF), HALF)]
        mid[core, rc * RC:(rc + 1) * RC] = (residual.astype(F32) + total).astype(BF16)
        copy1_out(rc, core).start()
    for rc in range(NRC):
        copy1_out(rc, 1 - core).wait_recv()

    hidden = jnp.concatenate([mid[0], mid[1]], axis=1)
    normed = norm_rows(hidden.astype(F32), gm[layer:layer + 1, :])
    for j in range(NCH):
        load(0, j).wait()
        gate = jnp.dot(normed, wg[j], preferred_element_type=F32)
        load(1, j).wait()
        up = jnp.dot(normed, wu[j], preferred_element_type=F32)
        act[:, j * CW:(j + 1) * CW] = (gate * jax.nn.sigmoid(gate) * up).astype(BF16)
    for j in range(NCH):
        load(2, j).wait()

    def copy2(j):
        return remote(send2.at[j], recv2.at[j], sems2, 0, j, sibling)

    def copy2_peer(j):
        return remote(pair2.at[j], peer2.at[j], sems2, 1, j, peer)

    def copy2_out(j, half):
        return remote(last.at[half * 2 + j], last.at[half * 2 + j], sems2, 2, j, sibling)

    def down(j):
        return jnp.dot(act[...], wd[j], preferred_element_type=F32)

    def to_sibling2(j):
        send2[j] = down(2 - core * 2 + j).astype(BF16)
        copy2(j).start()

    def to_peer2(j, own):
        copy2(j).wait_recv()
        pair2[j] = (own + recv2[j].astype(F32)).astype(BF16)
        copy2_peer(j).start()

    to_sibling2(0)
    own = down(core * 2)
    to_sibling2(1)
    to_peer2(0, own)
    to_peer2(1, down(core * 2 + 1))
    for j in range(2):
        copy2_peer(j).wait_recv()
        total = pair2[j].astype(F32) + peer2[j].astype(F32)
        last[core * 2 + j] = (mid[core, :, j * CW:(j + 1) * CW].astype(F32) + total).astype(BF16)
        copy2_out(j, core).start()
    for j in range(2):
        copy2_out(j, 1 - core).wait_recv()
    for j in range(NCH):
        out_ref[:, j * CW:(j + 1) * CW] = last[j]
    for rc in range(NRC):
        copy1(rc).wait_send()
        copy1_peer(rc).wait_send()
        copy1_out(rc, core).wait_send()
    for j in range(2):
        copy2(j).wait_send()
        copy2_peer(j).wait_send()
        copy2_out(j, core).wait_send()


def layer_call(layer, seq_lens, freq, hidden, g_attn, g_mlp, w_q, w_k, w_v, w_o, w_gate, w_up, w_down, k_cache, v_cache):
    tile = pltpu.VMEM((ROWS, KVD, SMAX), BF16)
    chunk1 = pltpu.VMEM((NRC, RC, HALF), BF16)
    chunk2 = pltpu.VMEM((2, ROWS, CW), BF16)
    return pl.pallas_call(
        functools.partial(layer_kernel, layer),
        out_shape=(jax.ShapeDtypeStruct((ROWS, D), BF16), tile, tile),
        in_specs=[HBM] * 15,
        out_specs=(VMEM, VMEM, VMEM),
        scratch_shapes=[
            pltpu.SMEM((1, ROWS), jnp.int32),
            pltpu.VMEM((1, ROWS), jnp.int32),
            pltpu.VMEM((1, 128), F32),
            pltpu.VMEM((ROWS, D), BF16),
            pltpu.VMEM(g_attn.shape, BF16),
            pltpu.VMEM(g_mlp.shape, BF16),
            pltpu.VMEM((D, QD), BF16),
            pltpu.VMEM((D, KVD), BF16),
            pltpu.VMEM((D, KVD), BF16),
            pltpu.VMEM((2, QD, HALF), BF16),
            pltpu.VMEM((NCH, D, CW), BF16),
            pltpu.VMEM((NCH, D, CW), BF16),
            pltpu.VMEM((NCH, FF, CW), BF16),
            pltpu.VMEM((KVD, ROWS), F32),
            pltpu.VMEM((KVD, ROWS), F32),
            pltpu.VMEM((ROWS * 8, 128), F32),
            pltpu.VMEM((ROWS * 8, 128), F32),
            pltpu.VMEM((NRC, RC, HALF), F32),
            chunk1, chunk1, chunk1, chunk1,
            pltpu.VMEM((2, ROWS, HALF), BF16),
            chunk2, chunk2, chunk2, chunk2,
            pltpu.VMEM((NCH, ROWS, CW), BF16),
            pltpu.VMEM((ROWS, FF), BF16),
            pltpu.SemaphoreType.DMA((9,)),
            pltpu.SemaphoreType.DMA((STEPS,)),
            pltpu.SemaphoreType.DMA((STEPS,)),
            pltpu.SemaphoreType.DMA((2,)),
            pltpu.SemaphoreType.DMA((3, NCH)),
            pltpu.SemaphoreType.DMA((6, NRC)),
            pltpu.SemaphoreType.DMA((6, 2)),
        ],
        compiler_params=pltpu.CompilerParams(vmem_limit_bytes=44 * 2 ** 20, collective_id=layer, has_side_effects=True),
        name=f"layer{layer}",
    )(seq_lens, seq_lens, freq, hidden, g_attn, g_mlp, w_q, w_k, w_v, w_o, w_gate, w_up, w_down, k_cache, v_cache)


def write_kernel(layer, aliased, *refs):
    k_ref, v_ref = refs[:2]
    ko_hbm, vo_hbm, sem = refs[4 if aliased else 2:]

    def store(n, i):
        src, dst = ((k_ref, ko_hbm), (v_ref, vo_hbm))[n]
        part = pl.ds(i * SEQS, SEQS)
        return pltpu.make_async_copy(src.at[part], dst.at[layer, part], sem.at[n, i])

    for i in range(STEPS):
        store(0, i).start()
        store(1, i).start()
    for i in range(STEPS):
        store(0, i).wait()
        store(1, i).wait()


def write_call(layer, layers, k_tile, v_tile, outs):
    cache = jax.ShapeDtypeStruct((layers, ROWS, KVD, SMAX), BF16)
    k_tile, v_tile = (pltpu.with_memory_space_constraint(x, pltpu.VMEM) for x in (k_tile, v_tile))
    return pl.pallas_call(
        functools.partial(write_kernel, layer, bool(outs)),
        out_shape=(cache, cache),
        in_specs=[VMEM, VMEM] + [HBM] * len(outs),
        out_specs=(HBM, HBM),
        scratch_shapes=[pltpu.SemaphoreType.DMA((2, STEPS))],
        input_output_aliases={2: 0, 3: 1} if outs else {},
        compiler_params=pltpu.CompilerParams(vmem_limit_bytes=2 ** 20),
        name=f"write{layer}",
    )(k_tile, v_tile, *outs)


def solution(mesh):
    cache_spec = P(None, "dp", None, "tp", None)
    col_spec = P(None, None, "tp")
    row_spec = P(None, "tp", None)
    in_specs = (P("dp", None), P("dp"), cache_spec, cache_spec, P(None, None), col_spec, col_spec, col_spec,
                row_spec, P(None, None), col_spec, col_spec, row_spec)
    out_specs = (P("dp", None), cache_spec, cache_spec)

    def local_step(hidden, seq_lens, k_cache, v_cache, g_attn, w_q, w_k, w_v, w_o, g_mlp, w_gate, w_up, w_down):
        layers = k_cache.shape[0]
        kt = k_cache.transpose(0, 1, 3, 4, 2).reshape(layers, ROWS, KVD, SMAX)
        vt = v_cache.transpose(0, 1, 3, 4, 2).reshape(layers, ROWS, KVD, SMAX)
        freq = jnp.asarray(np.tile(rope_freqs(HEAD), 4)[None, :])
        seq_row = seq_lens.reshape(1, ROWS)
        hidden, g_attn, w_q, w_k, w_v, w_o, g_mlp, w_gate, w_up, w_down, kt, vt, freq, seq_row = (
            pltpu.with_memory_space_constraint(x, pltpu.HBM)
            for x in (hidden, g_attn, w_q, w_k, w_v, w_o, g_mlp, w_gate, w_up, w_down, kt, vt, freq, seq_row))
        outs = ()
        for layer in range(layers):
            hidden, k_tile, v_tile = layer_call(layer, seq_row, freq, hidden, g_attn, g_mlp, w_q, w_k, w_v, w_o, w_gate, w_up,
                                                w_down, kt, vt)
            outs = write_call(layer, layers, k_tile, v_tile, outs)
            hidden, outs = lax.optimization_barrier((hidden, outs))

        def back(cache):
            return cache.reshape(layers, ROWS, 2, HEAD, SMAX).transpose(0, 1, 4, 2, 3)

        return hidden, back(outs[0]), back(outs[1])

    return jax.shard_map(local_step, mesh=mesh, in_specs=in_specs, out_specs=out_specs, check_vma=False)
```

time: 86.9 us -> 90.3 us (1.039)
  Pallas kernels: 85.3 us -> 88.7 us
    pallas_call x4, Pallas kernels: 85.3 us -> 88.7 us  [the longest x2 76.8 us: layer_call(): pl.pallas_call(functools.partial(layer_kernel, layer), out_shape=(jax.Sha...]
where the time goes in v3:
time: 90.3 us; the launch traced here: 90.2 us
  Pallas kernels  88.7 us (98%)
    pallas_call x2, Pallas kernels, layer_call(): pl.pallas_call(functools.partial(layer_kernel, layer), out_shape=(jax.Sha...  76.8 us
    pallas_call x2, Pallas kernels, write_call(): pl.pallas_call(functools.partial(write_kernel, layer, bool(outs)), out_sh...  11.9 us

profile of v3, /device:TPU:0, one launch (start us, length us, event | category | flops | bytes accessed | tf_op | source)
XLA Modules:
  0.0 90.2 jit_solution(3811255388035505673)
XLA Ops:
  0.6 38.6 %layer0.1 = (bf16[128,2048]{1,0:T(8,128)(2,1)}, bf16[128,128,256]{2,1,0:T(8,128)(2,1)S(1)}, bf16[128,128,256]{2,1,0:T(8,128)(2,1)S(1)}) custom-call(s32[1,128]{1,0:T(1,128)} %bitcast.19, s32[1,128]{1,0:T(1,128)} %bitcast.20, f32[1,128]{1,0:T(1,128)} %constant.2.clone.freq_hbm, bf16[128,2048]{1,0:T(8,128)(2,1)} %h_hbm.1, bf16[2,2048]{1,0:T(2,128)(2,1)} %ga_hbm.3, ...), custom_call_target="tpu_custom_call" | custom-call | tf_op jit(solution)/shard_map/layer0/pallas_call | solution.py:302
  39.3 6.0 %write0.1 = (bf16[2,128,128,256]{3,2,1,0:T(8,128)(2,1)}, bf16[2,128,128,256]{3,2,1,0:T(8,128)(2,1)}) custom-call(bf16[128,128,256]{2,1,0:T(8,128)(2,1)S(1)} %get-tuple-element.20.refs_0_, bf16[128,128,256]{2,1,0:T(8,128)(2,1)S(1)} %get-tuple-element.21.refs_1_), custom_call_target="tpu_custom_call" | custom-call | tf_op jit(solution)/shard_map/write0/pallas_call | solution.py:364
  45.2 38.2 %layer1.1 = (bf16[128,2048]{1,0:T(8,128)(2,1)}, bf16[128,128,256]{2,1,0:T(8,128)(2,1)S(1)}, bf16[128,128,256]{2,1,0:T(8,128)(2,1)S(1)}) custom-call(s32[1,128]{1,0:T(1,128)} %bitcast.21, s32[1,128]{1,0:T(1,128)} %bitcast.22, f32[1,128]{1,0:T(1,128)} %constant.2.clone.freq_hbm, bf16[128,2048]{1,0:T(8,128)(2,1)} %get-tuple-element.24.h_hbm, ...), custom_call_target="tpu_custom_call" | custom-call | tf_op jit(solution)/shard_map/layer1/pallas_call | solution.py:302
  83.4 0.0 copy-start
  83.4 6.0 %write1.1 = (bf16[2,128,128,256]{3,2,1,0:T(8,128)(2,1)}, bf16[2,128,128,256]{3,2,1,0:T(8,128)(2,1)}) custom-call(bf16[128,128,256]{2,1,0:T(8,128)(2,1)S(1)} %get-tuple-element.26.refs_0_, bf16[128,128,256]{2,1,0:T(8,128)(2,1)S(1)} %get-tuple-element.27.refs_1_, ...), custom_call_target="tpu_custom_call", output_to_operand_aliasing={{0}: (2, {}), {1}: (3, {})} | custom-call | tf_op jit(solution)/shard_map/write1/pallas_call | solution.py:364
  89.4 0.0 copy-done
  89.4 0.8 copy.22
Async XLA Ops:
  83.4 6.0 %copy-start = (bf16[128,2048]{1,0:T(8,128)(2,1)S(1)}, bf16[128,2048]{1,0:T(8,128)(2,1)}, u32[]{:S(2)}) copy-start(bf16[128,2048]{1,0:T(8,128)(2,1)} %get-tuple-element.38) | copy-start | bytes 1572868

commit v4 on v3

--- a/solution.py
+++ b/solution.py
@@ -29,6 +29,7 @@
 HALF = D // 2
 RC = 32
 NRC = ROWS // RC
+AHEAD = 3
 F32 = jnp.float32
 BF16 = jnp.bfloat16
 MESH = pl.DeviceIdType.MESH
@@ -94,8 +95,9 @@
 
     for i in range(9):
         small(i).start()
-    load_k(0).start()
-    load_v(0).start()
+    for i in range(AHEAD):
+        load_k(i).start()
+        load_v(i).start()
 
     small(0).wait()
     small(1).wait()
@@ -110,12 +112,6 @@
     small(4).wait()
     small(5).wait()
     small(6).wait()
-    for i in range(1, STEPS):
-        load_k(i).start()
-        load_v(i).start()
-        if i == 2:
-            load_o(0).start()
-            load_o(1).start()
     knew[...] = rope_slab(jnp.dot(normed, wk[...], preferred_element_type=F32), cos, sin).astype(BF16).astype(F32).T
     vnew[...] = jnp.dot(normed, wv[...], preferred_element_type=F32).astype(BF16).astype(F32).T
     for slab_idx in range(4):
@@ -133,6 +129,17 @@
     def attend(i):
         load_k(i).wait()
         load_v(i).wait()
+
+        @pl.when(i + AHEAD < STEPS)
+        def _():
+            load_k(i + AHEAD).start()
+            load_v(i + AHEAD).start()
+
+        @pl.when(i == 0)
+        def _():
+            load_o(0).start()
+            load_o(1).start()
+
         lane16 = lax.broadcasted_iota(jnp.int16, (KVD, SMAX), 1)
         lane8 = lax.broadcasted_iota(jnp.int32, (8, SMAX), 1)
         row16 = lax.broadcasted_iota(jnp.int32, (16, 128), 0)
@@ -215,27 +222,25 @@
         def _():
             to_peer1(rc - 1)
 
-        @pl.when(rc == 1)
-        def _():
-            for j in range(NCH):
-                load(0, j).start()
-                load(1, j).start()
-
-        @pl.when(rc == 2)
-        def _():
-            for j in range(NCH):
-                load(2, j).start()
-
         return carry
 
     lax.fori_loop(0, NRC, row_chunk, 0)
+    load(0, 0).start()
+    load(1, 0).start()
     to_peer1(NRC - 1)
+    load(0, 1).start()
+    load(1, 1).start()
     for rc in range(NRC):
         copy1_peer(rc).wait_recv()
         total = pair1[rc].astype(F32) + peer1[rc].astype(F32)
         residual = h_ref[rc * RC:(rc + 1) * RC, pl.ds(pl.multiple_of(core * HALF, HALF), HALF)]
         mid[core, rc * RC:(rc + 1) * RC] = (residual.astype(F32) + total).astype(BF16)
         copy1_out(rc, core).start()
+        if rc < 2:
+            load(0, rc + 2).start()
+            load(1, rc + 2).start()
+    for j in range(NCH):
+        load(2, j).start()
     for rc in range(NRC):
         copy1_out(rc, 1 - core).wait_recv()
 

time: 90.3 us -> 87.1 us (0.965)
  Pallas kernels: 88.7 us -> 85.4 us
    pallas_call x2, Pallas kernels: 76.8 us -> 73.5 us  [layer_call(): pl.pallas_call(functools.partial(layer_kernel, layer), out_shape=(jax.Sha...]
where the time goes in v4:
time: 87.1 us; the launch traced here: 86.9 us
  Pallas kernels  85.4 us (98%)
    pallas_call x2, Pallas kernels, layer_call(): pl.pallas_call(functools.partial(layer_kernel, layer), out_shape=(jax.Sha...  73.5 us
    pallas_call x2, Pallas kernels, write_call(): pl.pallas_call(functools.partial(write_kernel, layer, bool(outs)), out_sh...  11.9 us

profile of v4, /device:TPU:0, one launch (start us, length us, event | category | flops | bytes accessed | tf_op | source)
XLA Modules:
  0.0 86.9 jit_solution(6106560355300601798)
XLA Ops:
  0.6 37.6 %layer0.1 = (bf16[128,2048]{1,0:T(8,128)(2,1)}, bf16[128,128,256]{2,1,0:T(8,128)(2,1)S(1)}, bf16[128,128,256]{2,1,0:T(8,128)(2,1)S(1)}) custom-call(s32[1,128]{1,0:T(1,128)} %bitcast.19, s32[1,128]{1,0:T(1,128)} %bitcast.20, f32[1,128]{1,0:T(1,128)} %constant.2.clone.freq_hbm, bf16[128,2048]{1,0:T(8,128)(2,1)} %h_hbm.1, bf16[2,2048]{1,0:T(2,128)(2,1)} %ga_hbm.3, ...), custom_call_target="tpu_custom_call" | custom-call | tf_op jit(solution)/shard_map/layer0/pallas_call | solution.py:307
  38.2 6.0 %write0.1 = (bf16[2,128,128,256]{3,2,1,0:T(8,128)(2,1)}, bf16[2,128,128,256]{3,2,1,0:T(8,128)(2,1)}) custom-call(bf16[128,128,256]{2,1,0:T(8,128)(2,1)S(1)} %get-tuple-element.20.refs_0_, bf16[128,128,256]{2,1,0:T(8,128)(2,1)S(1)} %get-tuple-element.21.refs_1_), custom_call_target="tpu_custom_call" | custom-call | tf_op jit(solution)/shard_map/write0/pallas_call | solution.py:369
  44.2 35.9 %layer1.1 = (bf16[128,2048]{1,0:T(8,128)(2,1)}, bf16[128,128,256]{2,1,0:T(8,128)(2,1)S(1)}, bf16[128,128,256]{2,1,0:T(8,128)(2,1)S(1)}) custom-call(s32[1,128]{1,0:T(1,128)} %bitcast.21, s32[1,128]{1,0:T(1,128)} %bitcast.22, f32[1,128]{1,0:T(1,128)} %constant.2.clone.freq_hbm, bf16[128,2048]{1,0:T(8,128)(2,1)} %get-tuple-element.24.h_hbm, ...), custom_call_target="tpu_custom_call" | custom-call | tf_op jit(solution)/shard_map/layer1/pallas_call | solution.py:307
  80.1 0.0 copy-start
  80.1 6.0 %write1.1 = (bf16[2,128,128,256]{3,2,1,0:T(8,128)(2,1)}, bf16[2,128,128,256]{3,2,1,0:T(8,128)(2,1)}) custom-call(bf16[128,128,256]{2,1,0:T(8,128)(2,1)S(1)} %get-tuple-element.26.refs_0_, bf16[128,128,256]{2,1,0:T(8,128)(2,1)S(1)} %get-tuple-element.27.refs_1_, ...), custom_call_target="tpu_custom_call", output_to_operand_aliasing={{0}: (2, {}), {1}: (3, {})} | custom-call | tf_op jit(solution)/shard_map/write1/pallas_call | solution.py:369
  86.1 0.0 copy-done
  86.1 0.8 copy.22
Async XLA Ops:
  80.1 6.0 %copy-start = (bf16[128,2048]{1,0:T(8,128)(2,1)S(1)}, bf16[128,2048]{1,0:T(8,128)(2,1)}, u32[]{:S(2)}) copy-start(bf16[128,2048]{1,0:T(8,128)(2,1)} %get-tuple-element.38) | copy-start | bytes 1572868

commit v5 on v4

--- a/solution.py
+++ b/solution.py
@@ -82,12 +82,15 @@
     def load_v(i):
         return pltpu.make_async_copy(v_hbm.at[layer, pl.ds(i * SEQS, SEQS)], vbuf.at[pl.ds(i * SEQS, SEQS)], vsem.at[i])
 
-    def load_o(j):
-        return pltpu.make_async_copy(wo_hbm.at[layer, :, pl.ds(j * HALF, HALF)], wo.at[j], osem.at[j])
+    def load_o():
+        return pltpu.make_async_copy(wo_hbm.at[layer], wo, osem.at[0])
 
     def load(kind, j):
-        src = (wg_hbm, wu_hbm, wd_hbm)[kind].at[layer, :, pl.ds(j * CW, CW)]
-        return pltpu.make_async_copy(src, (wg, wu, wd)[kind].at[j], wsem.at[kind, j])
+        part = pl.ds(j * CW, CW)
+        return pltpu.make_async_copy((wg_hbm, wu_hbm, wd_hbm)[kind].at[layer, part], (wg, wu, wd)[kind].at[part], wsem.at[kind, j])
+
+    def half_cols(half):
+        return pl.ds(pl.multiple_of(half * HALF, HALF), HALF)
 
     def remote(src, dst, sems, i, j, to):
         return pltpu.make_async_remote_copy(src_ref=src, dst_ref=dst, send_sem=sems.at[2 * i, j], recv_sem=sems.at[2 * i + 1, j],
@@ -137,8 +140,7 @@
 
         @pl.when(i == 0)
         def _():
-            load_o(0).start()
-            load_o(1).start()
+            load_o().start()
 
         lane16 = lax.broadcasted_iota(jnp.int16, (KVD, SMAX), 1)
         lane8 = lax.broadcasted_iota(jnp.int32, (8, SMAX), 1)
@@ -211,12 +213,11 @@
 
         @pl.when(rc == 0)
         def _():
-            load_o(0).wait()
-            load_o(1).wait()
-
-        send1[rc] = jnp.dot(attn, wo[1 - core], preferred_element_type=F32).astype(BF16)
+            load_o().wait()
+
+        send1[rc] = jnp.dot(attn, wo[:, half_cols(1 - core)], preferred_element_type=F32).astype(BF16)
         copy1(rc).start()
-        own1[rc] = jnp.dot(attn, wo[core], preferred_element_type=F32)
+        own1[rc] = jnp.dot(attn, wo[:, half_cols(core)], preferred_element_type=F32)
 
         @pl.when(rc > 0)
         def _():
@@ -233,7 +234,7 @@
     for rc in range(NRC):
         copy1_peer(rc).wait_recv()
         total = pair1[rc].astype(F32) + peer1[rc].astype(F32)
-        residual = h_ref[rc * RC:(rc + 1) * RC, pl.ds(pl.multiple_of(core * HALF, HALF), HALF)]
+        residual = h_ref[rc * RC:(rc + 1) * RC, half_cols(core)]
         mid[core, rc * RC:(rc + 1) * RC] = (residual.astype(F32) + total).astype(BF16)
         copy1_out(rc, core).start()
         if rc < 2:
@@ -248,9 +249,10 @@
     normed = norm_rows(hidden.astype(F32), gm[layer:layer + 1, :])
     for j in range(NCH):
         load(0, j).wait()
-        gate = jnp.dot(normed, wg[j], preferred_element_type=F32)
         load(1, j).wait()
-        up = jnp.dot(normed, wu[j], preferred_element_type=F32)
+    for j in range(NCH):
+        gate = jnp.dot(normed, wg[:, j * CW:(j + 1) * CW], preferred_element_type=F32)
+        up = jnp.dot(normed, wu[:, j * CW:(j + 1) * CW], preferred_element_type=F32)
         act[:, j * CW:(j + 1) * CW] = (gate * jax.nn.sigmoid(gate) * up).astype(BF16)
     for j in range(NCH):
         load(2, j).wait()
@@ -265,7 +267,7 @@
         return remote(last.at[half * 2 + j], last.at[half * 2 + j], sems2, 2, j, sibling)
 
     def down(j):
-        return jnp.dot(act[...], wd[j], preferred_element_type=F32)
+        return jnp.dot(act[...], wd[:, pl.ds(pl.multiple_of(j * CW, CW), CW)], preferred_element_type=F32)
 
     def to_sibling2(j):
         send2[j] = down(2 - core * 2 + j).astype(BF16)
@@ -319,10 +321,10 @@
             pltpu.VMEM((D, QD), BF16),
             pltpu.VMEM((D, KVD), BF16),
             pltpu.VMEM((D, KVD), BF16),
-            pltpu.VMEM((2, QD, HALF), BF16),
-            pltpu.VMEM((NCH, D, CW), BF16),
-            pltpu.VMEM((NCH, D, CW), BF16),
-            pltpu.VMEM((NCH, FF, CW), BF16),
+            pltpu.VMEM((QD, D), BF16),
+            pltpu.VMEM((D, FF), BF16),
+            pltpu.VMEM((D, FF), BF16),
+            pltpu.VMEM((FF, D), BF16),
             pltpu.VMEM((KVD, ROWS), F32),
             pltpu.VMEM((KVD, ROWS), F32),
             pltpu.VMEM((ROWS * 8, 128), F32),
@@ -336,7 +338,7 @@
             pltpu.SemaphoreType.DMA((9,)),
             pltpu.SemaphoreType.DMA((STEPS,)),
             pltpu.SemaphoreType.DMA((STEPS,)),
-            pltpu.SemaphoreType.DMA((2,)),
+            pltpu.SemaphoreType.DMA((1,)),
             pltpu.SemaphoreType.DMA((3, NCH)),
             pltpu.SemaphoreType.DMA((6, NRC)),
             pltpu.SemaphoreType.DMA((6, 2)),

time: 87.1 us -> 86.1 us (0.989)
  Pallas kernels: 85.4 us -> 84.5 us
    pallas_call x2, Pallas kernels: 73.5 us -> 72.6 us  [layer_call(): pl.pallas_call(functools.partial(layer_kernel, layer), out_shape=(jax.Sha...]
where the time goes in v5:
time: 86.1 us; the launch traced here: 86 us
  Pallas kernels  84.5 us (98%)
    pallas_call x2, Pallas kernels, layer_call(): pl.pallas_call(functools.partial(layer_kernel, layer), out_shape=(jax.Sha...  72.6 us
    pallas_call x2, Pallas kernels, write_call(): pl.pallas_call(functools.partial(write_kernel, layer, bool(outs)), out_sh...  11.9 us

profile of v5, /device:TPU:0, one launch (start us, length us, event | category | flops | bytes accessed | tf_op | source)
XLA Modules:
  0.0 86.0 jit_solution(6843631178026455558)
XLA Ops:
  0.6 37.5 %layer0.1 = (bf16[128,2048]{1,0:T(8,128)(2,1)}, bf16[128,128,256]{2,1,0:T(8,128)(2,1)S(1)}, bf16[128,128,256]{2,1,0:T(8,128)(2,1)S(1)}) custom-call(s32[1,128]{1,0:T(1,128)} %bitcast.19, s32[1,128]{1,0:T(1,128)} %bitcast.20, f32[1,128]{1,0:T(1,128)} %constant.2.clone.freq_hbm, bf16[128,2048]{1,0:T(8,128)(2,1)} %h_hbm.1, bf16[2,2048]{1,0:T(2,128)(2,1)} %ga_hbm.3, ...), custom_call_target="tpu_custom_call" | custom-call | tf_op jit(solution)/shard_map/layer0/pallas_call | solution.py:309
  38.1 6.0 %write0.1 = (bf16[2,128,128,256]{3,2,1,0:T(8,128)(2,1)}, bf16[2,128,128,256]{3,2,1,0:T(8,128)(2,1)}) custom-call(bf16[128,128,256]{2,1,0:T(8,128)(2,1)S(1)} %get-tuple-element.20.refs_0_, bf16[128,128,256]{2,1,0:T(8,128)(2,1)S(1)} %get-tuple-element.21.refs_1_), custom_call_target="tpu_custom_call" | custom-call | tf_op jit(solution)/shard_map/write0/pallas_call | solution.py:371
  44.1 35.1 %layer1.1 = (bf16[128,2048]{1,0:T(8,128)(2,1)}, bf16[128,128,256]{2,1,0:T(8,128)(2,1)S(1)}, bf16[128,128,256]{2,1,0:T(8,128)(2,1)S(1)}) custom-call(s32[1,128]{1,0:T(1,128)} %bitcast.21, s32[1,128]{1,0:T(1,128)} %bitcast.22, f32[1,128]{1,0:T(1,128)} %constant.2.clone.freq_hbm, bf16[128,2048]{1,0:T(8,128)(2,1)} %get-tuple-element.24.h_hbm, ...), custom_call_target="tpu_custom_call" | custom-call | tf_op jit(solution)/shard_map/layer1/pallas_call | solution.py:309
  79.2 0.0 copy-start
  79.2 6.0 %write1.1 = (bf16[2,128,128,256]{3,2,1,0:T(8,128)(2,1)}, bf16[2,128,128,256]{3,2,1,0:T(8,128)(2,1)}) custom-call(bf16[128,128,256]{2,1,0:T(8,128)(2,1)S(1)} %get-tuple-element.26.refs_0_, bf16[128,128,256]{2,1,0:T(8,128)(2,1)S(1)} %get-tuple-element.27.refs_1_, ...), custom_call_target="tpu_custom_call", output_to_operand_aliasing={{0}: (2, {}), {1}: (3, {})} | custom-call | tf_op jit(solution)/shard_map/write1/pallas_call | solution.py:371
  85.2 0.0 copy-done
  85.2 0.8 copy.22
Async XLA Ops:
  79.2 6.0 %copy-start = (bf16[128,2048]{1,0:T(8,128)(2,1)S(1)}, bf16[128,2048]{1,0:T(8,128)(2,1)}, u32[]{:S(2)}) copy-start(bf16[128,2048]{1,0:T(8,128)(2,1)} %get-tuple-element.38) | copy-start | bytes 1572868

commit v6 on v5

--- a/solution.py
+++ b/solution.py
@@ -60,7 +60,7 @@
 
 def layer_kernel(layer, seq_hbm, seqv_hbm, freq_hbm, h_hbm, ga_hbm, gm_hbm, wq_hbm, wk_hbm, wv_hbm, wo_hbm, wg_hbm, wu_hbm,
                  wd_hbm, k_hbm, v_hbm, out_ref, kbuf, vbuf, seq_ref, seqv, freq, h_ref, ga, gm, wq, wk, wv, wo, wg, wu, wd,
-                 knew, vnew, qrow, orow, own1, send1, recv1, pair1, peer1, mid, send2, recv2, pair2, peer2, last, act,
+                 knew, vnew, krow, vrow, qrow, orow, own1, send1, recv1, pair1, peer1, mid, send2, recv2, pair2, peer2, last, act,
                  sem, ksem, vsem, osem, wsem, sems1, sems2):
     me = lax.axis_index("tp")
     core = lax.rem(me, 2)
@@ -98,10 +98,6 @@
 
     for i in range(9):
         small(i).start()
-    for i in range(AHEAD):
-        load_k(i).start()
-        load_v(i).start()
-
     small(0).wait()
     small(1).wait()
     angle = jnp.broadcast_to(seqv[...].astype(F32), (ROWS, 128)).T * freq[...]
@@ -115,8 +111,15 @@
     small(4).wait()
     small(5).wait()
     small(6).wait()
-    knew[...] = rope_slab(jnp.dot(normed, wk[...], preferred_element_type=F32), cos, sin).astype(BF16).astype(F32).T
-    vnew[...] = jnp.dot(normed, wv[...], preferred_element_type=F32).astype(BF16).astype(F32).T
+    for i in range(AHEAD):
+        load_k(i).start()
+        load_v(i).start()
+    k_row = rope_slab(jnp.dot(normed, wk[...], preferred_element_type=F32), cos, sin).astype(BF16).astype(F32)
+    v_row = jnp.dot(normed, wv[...], preferred_element_type=F32).astype(BF16).astype(F32)
+    krow[...] = k_row
+    vrow[...] = v_row
+    knew[...] = k_row.T
+    vnew[...] = v_row.T
     for slab_idx in range(4):
         slab = jnp.dot(normed, wq[:, slab_idx * 128:(slab_idx + 1) * 128], preferred_element_type=F32)
         slab = rope_slab(slab, cos, sin).astype(BF16).astype(F32)
@@ -142,43 +145,52 @@
         def _():
             load_o().start()
 
-        lane16 = lax.broadcasted_iota(jnp.int16, (KVD, SMAX), 1)
         lane8 = lax.broadcasted_iota(jnp.int32, (8, SMAX), 1)
         row16 = lax.broadcasted_iota(jnp.int32, (16, 128), 0)
         row8 = lax.broadcasted_iota(jnp.int32, (8, 128), 0)
         lane_o = lax.broadcasted_iota(jnp.int32, (8, 128), 1)
+        scale = HEAD ** -0.5
+        scores = []
+        fresh = []
+        for p in range(SEQS // 2):
+            b = i * SEQS + 2 * p
+            q2 = qrow[pl.ds(b * 8, 16), :]
+            qb = jnp.concatenate([jnp.where(row16 < 8, q2, 0.0), jnp.where(row16 >= 8, q2, 0.0)], axis=1).astype(BF16)
+            kk = kbuf[pl.ds(b, 2)].reshape(2 * KVD, SMAX)
+            scores.append(jnp.dot(qb, kk, preferred_element_type=F32) * scale)
+            for j in range(2):
+                fresh.append(jnp.sum(q2[8 * j:8 * j + 8] * krow[pl.ds(b + j, 1), :], axis=-1, keepdims=True) * scale)
+        for p in range(SEQS // 2):
+            b = i * SEQS + 2 * p
+            halves = []
+            added = []
+            for j in range(2):
+                s = jnp.where(lane8 < seq_ref[0, b + j], scores[p][8 * j:8 * j + 8], -1e30)
+                s_new = fresh[2 * p + j]
+                peak = jnp.maximum(jnp.max(s, axis=-1, keepdims=True), s_new)
+                e = jnp.exp(s - peak)
+                e_new = jnp.exp(s_new - peak)
+                denom = jnp.sum(e, axis=-1, keepdims=True) + e_new
+                halves.append(e / denom)
+                added.append((e_new / denom).astype(BF16).astype(F32) * vrow[pl.ds(b + j, 1), :])
+            prob = jnp.concatenate(halves, axis=0).astype(BF16)
+            vv = vbuf[pl.ds(b, 2)].reshape(2 * KVD, SMAX)
+            mix = lax.dot_general(prob, vv, (((1,), (1,)), ((), ())), preferred_element_type=F32)
+            for j in range(2):
+                m = mix[8 * j:8 * j + 8, 128 * j:128 * j + 128] + added[j]
+                orow[pl.ds((b + j) * 8, 8), :] = jnp.where((row8 < 4) == (lane_o < HEAD), m, pltpu.roll(m, HEAD, 1))
+
+    def insert(i, carry):
+        lane16 = lax.broadcasted_iota(jnp.int16, (KVD, SMAX), 1)
         shift = lax.rem(ROWS - i * SEQS, ROWS)
-
-        def insert(buf, new_ref):
+        for buf, new_ref in ((kbuf, knew), (vbuf, vnew)):
             new = pltpu.roll(new_ref[...], shift, 1)
             for j in range(SEQS):
                 b = i * SEQS + j
                 column = jnp.broadcast_to(new[:, j:j + 1], (KVD, 128)).astype(BF16)
                 here = lane16 == seq_ref[0, b].astype(jnp.int16)
                 buf[b] = jnp.where(here, jnp.concatenate([column, column], axis=1), buf[b])
-
-        insert(kbuf, knew)
-        insert(vbuf, vnew)
-        scores = []
-        for p in range(SEQS // 2):
-            b = i * SEQS + 2 * p
-            q2 = qrow[pl.ds(b * 8, 16), :]
-            qb = jnp.concatenate([jnp.where(row16 < 8, q2, 0.0), jnp.where(row16 >= 8, q2, 0.0)], axis=1).astype(BF16)
-            kk = kbuf[pl.ds(b, 2)].reshape(2 * KVD, SMAX)
-            scores.append(jnp.dot(qb, kk, preferred_element_type=F32) * (HEAD ** -0.5))
-        for p in range(SEQS // 2):
-            b = i * SEQS + 2 * p
-            halves = []
-            for j in range(2):
-                s = jnp.where(lane8 <= seq_ref[0, b + j], scores[p][8 * j:8 * j + 8], -1e30)
-                e = jnp.exp(s - jnp.max(s, axis=-1, keepdims=True))
-                halves.append(e / jnp.sum(e, axis=-1, keepdims=True))
-            prob = jnp.concatenate(halves, axis=0).astype(BF16)
-            vv = vbuf[pl.ds(b, 2)].reshape(2 * KVD, SMAX)
-            mix = lax.dot_general(prob, vv, (((1,), (1,)), ((), ())), preferred_element_type=F32)
-            for j in range(2):
-                m = mix[8 * j:8 * j + 8, 128 * j:128 * j + 128]
-                orow[pl.ds((b + j) * 8, 8), :] = jnp.where((row8 < 4) == (lane_o < HEAD), m, pltpu.roll(m, HEAD, 1))
+        return carry
 
     def rows(rc):
         return pl.ds(pl.multiple_of(rc * RC, RC), RC)
@@ -223,25 +235,28 @@
         def _():
             to_peer1(rc - 1)
 
+        @pl.when(rc >= NRC - 2)
+        def _():
+            load(0, rc - NRC + 2).start()
+            load(1, rc - NRC + 2).start()
+
         return carry
 
     lax.fori_loop(0, NRC, row_chunk, 0)
-    load(0, 0).start()
-    load(1, 0).start()
+    load(0, 2).start()
+    load(1, 2).start()
+    lax.fori_loop(0, STEPS // 2, insert, 0)
     to_peer1(NRC - 1)
-    load(0, 1).start()
-    load(1, 1).start()
+    load(0, 3).start()
+    load(1, 3).start()
+    lax.fori_loop(STEPS // 2, STEPS, insert, 0)
     for rc in range(NRC):
         copy1_peer(rc).wait_recv()
         total = pair1[rc].astype(F32) + peer1[rc].astype(F32)
         residual = h_ref[rc * RC:(rc + 1) * RC, half_cols(core)]
         mid[core, rc * RC:(rc + 1) * RC] = (residual.astype(F32) + total).astype(BF16)
         copy1_out(rc, core).start()
-        if rc < 2:
-            load(0, rc + 2).start()
-            load(1, rc + 2).start()
-    for j in range(NCH):
-        load(2, j).start()
+        load(2, rc).start()
     for rc in range(NRC):
         copy1_out(rc, 1 - core).wait_recv()
 
@@ -327,6 +342,8 @@
             pltpu.VMEM((FF, D), BF16),
             pltpu.VMEM((KVD, ROWS), F32),
             pltpu.VMEM((KVD, ROWS), F32),
+            pltpu.VMEM((ROWS, KVD), F32),
+            pltpu.VMEM((ROWS, KVD), F32),
             pltpu.VMEM((ROWS * 8, 128), F32),
             pltpu.VMEM((ROWS * 8, 128), F32),
             pltpu.VMEM((NRC, RC, HALF), F32),

time: 86.1 us -> 85.3 us (level)
  no operation moved by 1% of the time
where the time goes in v6:
time: 85.3 us; the launch traced here: 85.2 us
  Pallas kernels  83.7 us (98%)
    pallas_call x2, Pallas kernels, layer_call(): pl.pallas_call(functools.partial(layer_kernel, layer), out_shape=(jax.Sha...  71.8 us
    pallas_call x2, Pallas kernels, write_call(): pl.pallas_call(functools.partial(write_kernel, layer, bool(outs)), out_sh...  11.9 us

profile of v6, /device:TPU:0, one launch (start us, length us, event | category | flops | bytes accessed | tf_op | source)
XLA Modules:
  0.0 85.2 jit_solution(7041120554075029031)
XLA Ops:
  0.6 36.4 %layer0.1 = (bf16[128,2048]{1,0:T(8,128)(2,1)}, bf16[128,128,256]{2,1,0:T(8,128)(2,1)S(1)}, bf16[128,128,256]{2,1,0:T(8,128)(2,1)S(1)}) custom-call(s32[1,128]{1,0:T(1,128)} %bitcast.19, s32[1,128]{1,0:T(1,128)} %bitcast.20, f32[1,128]{1,0:T(1,128)} %constant.2.clone.freq_hbm, bf16[128,2048]{1,0:T(8,128)(2,1)} %h_hbm.1, bf16[2,2048]{1,0:T(2,128)(2,1)} %ga_hbm.3, ...), custom_call_target="tpu_custom_call" | custom-call | tf_op jit(solution)/shard_map/layer0/pallas_call | solution.py:324
  37.0 6.0 %write0.1 = (bf16[2,128,128,256]{3,2,1,0:T(8,128)(2,1)}, bf16[2,128,128,256]{3,2,1,0:T(8,128)(2,1)}) custom-call(bf16[128,128,256]{2,1,0:T(8,128)(2,1)S(1)} %get-tuple-element.20.refs_0_, bf16[128,128,256]{2,1,0:T(8,128)(2,1)S(1)} %get-tuple-element.21.refs_1_), custom_call_target="tpu_custom_call" | custom-call | tf_op jit(solution)/shard_map/write0/pallas_call | solution.py:388
  43.0 35.4 %layer1.1 = (bf16[128,2048]{1,0:T(8,128)(2,1)}, bf16[128,128,256]{2,1,0:T(8,128)(2,1)S(1)}, bf16[128,128,256]{2,1,0:T(8,128)(2,1)S(1)}) custom-call(s32[1,128]{1,0:T(1,128)} %bitcast.21, s32[1,128]{1,0:T(1,128)} %bitcast.22, f32[1,128]{1,0:T(1,128)} %constant.2.clone.freq_hbm, bf16[128,2048]{1,0:T(8,128)(2,1)} %get-tuple-element.24.h_hbm, ...), custom_call_target="tpu_custom_call" | custom-call | tf_op jit(solution)/shard_map/layer1/pallas_call | solution.py:324
  78.4 0.0 copy-start
  78.4 6.0 %write1.1 = (bf16[2,128,128,256]{3,2,1,0:T(8,128)(2,1)}, bf16[2,128,128,256]{3,2,1,0:T(8,128)(2,1)}) custom-call(bf16[128,128,256]{2,1,0:T(8,128)(2,1)S(1)} %get-tuple-element.26.refs_0_, bf16[128,128,256]{2,1,0:T(8,128)(2,1)S(1)} %get-tuple-element.27.refs_1_, ...), custom_call_target="tpu_custom_call", output_to_operand_aliasing={{0}: (2, {}), {1}: (3, {})} | custom-call | tf_op jit(solution)/shard_map/write1/pallas_call | solution.py:388
  84.4 0.0 copy-done
  84.4 0.8 copy.22
Async XLA Ops:
  78.4 6.0 %copy-start = (bf16[128,2048]{1,0:T(8,128)(2,1)S(1)}, bf16[128,2048]{1,0:T(8,128)(2,1)}, u32[]{:S(2)}) copy-start(bf16[128,2048]{1,0:T(8,128)(2,1)} %get-tuple-element.38) | copy-start | bytes 1572868

commit v7 on v6

--- a/solution.py
+++ b/solution.py
@@ -98,6 +98,8 @@
 
     for i in range(9):
         small(i).start()
+    load_k(0).start()
+    load_v(0).start()
     small(0).wait()
     small(1).wait()
     angle = jnp.broadcast_to(seqv[...].astype(F32), (ROWS, 128)).T * freq[...]
@@ -110,8 +112,7 @@
     normed = norm_rows(h_ref[...].astype(F32), ga[layer:layer + 1, :])
     small(4).wait()
     small(5).wait()
-    small(6).wait()
-    for i in range(AHEAD):
+    for i in range(1, AHEAD):
         load_k(i).start()
         load_v(i).start()
     k_row = rope_slab(jnp.dot(normed, wk[...], preferred_element_type=F32), cos, sin).astype(BF16).astype(F32)
@@ -120,6 +121,7 @@
     vrow[...] = v_row
     knew[...] = k_row.T
     vnew[...] = v_row.T
+    small(6).wait()
     for slab_idx in range(4):
         slab = jnp.dot(normed, wq[:, slab_idx * 128:(slab_idx + 1) * 128], preferred_element_type=F32)
         slab = rope_slab(slab, cos, sin).astype(BF16).astype(F32)
@@ -235,28 +237,26 @@
         def _():
             to_peer1(rc - 1)
 
-        @pl.when(rc >= NRC - 2)
+        @pl.when(rc == NRC - 2)
         def _():
-            load(0, rc - NRC + 2).start()
-            load(1, rc - NRC + 2).start()
+            for j in range(NCH):
+                load(0, j).start()
+                load(1, j).start()
 
         return carry
 
     lax.fori_loop(0, NRC, row_chunk, 0)
-    load(0, 2).start()
-    load(1, 2).start()
-    lax.fori_loop(0, STEPS // 2, insert, 0)
+    for j in range(NCH):
+        load(2, j).start()
+    lax.fori_loop(0, 1, insert, 0)
     to_peer1(NRC - 1)
-    load(0, 3).start()
-    load(1, 3).start()
-    lax.fori_loop(STEPS // 2, STEPS, insert, 0)
+    lax.fori_loop(1, STEPS, insert, 0)
     for rc in range(NRC):
         copy1_peer(rc).wait_recv()
         total = pair1[rc].astype(F32) + peer1[rc].astype(F32)
         residual = h_ref[rc * RC:(rc + 1) * RC, half_cols(core)]
         mid[core, rc * RC:(rc + 1) * RC] = (residual.astype(F32) + total).astype(BF16)
         copy1_out(rc, core).start()
-        load(2, rc).start()
     for rc in range(NRC):
         copy1_out(rc, 1 - core).wait_recv()
 
@@ -317,13 +317,13 @@
         copy2_out(j, core).wait_send()
 
 
-def layer_call(layer, seq_lens, freq, hidden, g_attn, g_mlp, w_q, w_k, w_v, w_o, w_gate, w_up, w_down, k_cache, v_cache):
+def layer_call(layer, last, seq_lens, freq, hidden, g_attn, g_mlp, w_q, w_k, w_v, w_o, w_gate, w_up, w_down, k_cache, v_cache):
     tile = pltpu.VMEM((ROWS, KVD, SMAX), BF16)
     chunk1 = pltpu.VMEM((NRC, RC, HALF), BF16)
     chunk2 = pltpu.VMEM((2, ROWS, CW), BF16)
     return pl.pallas_call(
         functools.partial(layer_kernel, layer),
-        out_shape=(jax.ShapeDtypeStruct((ROWS, D), BF16), tile, tile),
+        out_shape=(pltpu.VMEM((ROWS, D), BF16) if last else jax.ShapeDtypeStruct((ROWS, D), BF16), tile, tile),
         in_specs=[HBM] * 15,
         out_specs=(VMEM, VMEM, VMEM),
         scratch_shapes=[
@@ -365,36 +365,35 @@
     )(seq_lens, seq_lens, freq, hidden, g_attn, g_mlp, w_q, w_k, w_v, w_o, w_gate, w_up, w_down, k_cache, v_cache)
 
 
-def write_kernel(layer, aliased, *refs):
-    k_ref, v_ref = refs[:2]
-    ko_hbm, vo_hbm, sem = refs[4 if aliased else 2:]
-
-    def store(n, i):
-        src, dst = ((k_ref, ko_hbm), (v_ref, vo_hbm))[n]
-        part = pl.ds(i * SEQS, SEQS)
-        return pltpu.make_async_copy(src.at[part], dst.at[layer, part], sem.at[n, i])
-
-    for i in range(STEPS):
-        store(0, i).start()
-        store(1, i).start()
-    for i in range(STEPS):
-        store(0, i).wait()
-        store(1, i).wait()
-
-
-def write_call(layer, layers, k_tile, v_tile, outs):
+def write_kernel(layer, n_in, *refs):
+    sources, results, sem = refs[:n_in], refs[-1 - n_in:-1], refs[-1]
+    copies = []
+    for n in range(2):
+        for i in range(STEPS):
+            part = pl.ds(i * SEQS, SEQS)
+            copies.append(pltpu.make_async_copy(sources[n].at[part], results[n].at[layer, part], sem.at[n, i]))
+    if n_in > 2:
+        copies.append(pltpu.make_async_copy(sources[2], results[2], sem.at[2, 0]))
+    for copy in copies:
+        copy.start()
+    for copy in copies:
+        copy.wait()
+
+
+def write_call(layer, layers, tiles, outs):
     cache = jax.ShapeDtypeStruct((layers, ROWS, KVD, SMAX), BF16)
-    k_tile, v_tile = (pltpu.with_memory_space_constraint(x, pltpu.VMEM) for x in (k_tile, v_tile))
+    n_in = len(tiles)
+    tiles = [pltpu.with_memory_space_constraint(x, pltpu.VMEM) for x in tiles]
     return pl.pallas_call(
-        functools.partial(write_kernel, layer, bool(outs)),
-        out_shape=(cache, cache),
-        in_specs=[VMEM, VMEM] + [HBM] * len(outs),
-        out_specs=(HBM, HBM),
-        scratch_shapes=[pltpu.SemaphoreType.DMA((2, STEPS))],
-        input_output_aliases={2: 0, 3: 1} if outs else {},
+        functools.partial(write_kernel, layer, n_in),
+        out_shape=(cache, cache, jax.ShapeDtypeStruct((ROWS, D), BF16))[:n_in],
+        in_specs=[VMEM] * n_in + [HBM] * len(outs),
+        out_specs=(HBM,) * n_in,
+        scratch_shapes=[pltpu.SemaphoreType.DMA((3, STEPS))],
+        input_output_aliases={n_in: 0, n_in + 1: 1} if outs else {},
         compiler_params=pltpu.CompilerParams(vmem_limit_bytes=2 ** 20),
         name=f"write{layer}",
-    )(k_tile, v_tile, *outs)
+    )(*tiles, *outs)
 
 
 def solution(mesh):
@@ -416,10 +415,13 @@
             for x in (hidden, g_attn, w_q, w_k, w_v, w_o, g_mlp, w_gate, w_up, w_down, kt, vt, freq, seq_row))
         outs = ()
         for layer in range(layers):
-            hidden, k_tile, v_tile = layer_call(layer, seq_row, freq, hidden, g_attn, g_mlp, w_q, w_k, w_v, w_o, w_gate, w_up,
+            hidden, k_tile, v_tile = layer_call(layer, layer == layers - 1, seq_row, freq, hidden, g_attn, g_mlp, w_q, w_k, w_v, w_o, w_gate, w_up,
                                                 w_down, kt, vt)
-            outs = write_call(layer, layers, k_tile, v_tile, outs)
-            hidden, outs = lax.optimization_barrier((hidden, outs))
+            if layer < layers - 1:
+                outs = write_call(layer, layers, (k_tile, v_tile), outs)
+                hidden, outs = lax.optimization_barrier((hidden, outs))
+            else:
+                *outs, hidden = write_call(layer, layers, (k_tile, v_tile, hidden), outs)
 
         def back(cache):
             return cache.reshape(layers, ROWS, 2, HEAD, SMAX).transpose(0, 1, 4, 2, 3)

time: 85.3 us -> 81.6 us (0.957)
  Pallas kernels: 83.7 us -> 80.6 us
    pallas_call x4, Pallas kernels: 83.7 us -> 80.6 us  [the longest x2 68.4 us: layer_call(): pl.pallas_call(functools.partial(layer_kernel, layer), out_shape=(pltpu.V...]
where the time goes in v7:
time: 81.6 us; the launch traced here: 81.4 us
  Pallas kernels  80.6 us (99%)
    pallas_call x2, Pallas kernels, layer_call(): pl.pallas_call(functools.partial(layer_kernel, layer), out_shape=(pltpu.V...  68.4 us
    pallas_call x2, Pallas kernels, write_call(): pl.pallas_call(functools.partial(write_kernel, layer, n_in), out_shape=(c...  12.2 us

profile of v7, /device:TPU:0, one launch (start us, length us, event | category | flops | bytes accessed | tf_op | source)
XLA Modules:
  0.0 81.4 jit_solution(2599757848629296399)
XLA Ops:
  0.6 35.9 %layer0.1 = (bf16[128,2048]{1,0:T(8,128)(2,1)}, bf16[128,128,256]{2,1,0:T(8,128)(2,1)S(1)}, bf16[128,128,256]{2,1,0:T(8,128)(2,1)S(1)}) custom-call(s32[1,128]{1,0:T(1,128)} %bitcast.19, s32[1,128]{1,0:T(1,128)} %bitcast.20, f32[1,128]{1,0:T(1,128)} %constant.2.clone.freq_hbm, bf16[128,2048]{1,0:T(8,128)(2,1)} %h_hbm.1, bf16[2,2048]{1,0:T(2,128)(2,1)} %ga_hbm.3, ...), custom_call_target="tpu_custom_call" | custom-call | tf_op jit(solution)/shard_map/layer0/pallas_call | solution.py:324
  36.6 6.0 %write0.1 = (bf16[2,128,128,256]{3,2,1,0:T(8,128)(2,1)}, bf16[2,128,128,256]{3,2,1,0:T(8,128)(2,1)}) custom-call(bf16[128,128,256]{2,1,0:T(8,128)(2,1)S(1)} %get-tuple-element.18.refs_0_, bf16[128,128,256]{2,1,0:T(8,128)(2,1)S(1)} %get-tuple-element.19.refs_1_), custom_call_target="tpu_custom_call" | custom-call | tf_op jit(solution)/shard_map/write0/pallas_call | solution.py:387
  42.6 32.5 %layer1.1 = (bf16[128,2048]{1,0:T(8,128)(2,1)S(1)}, bf16[128,128,256]{2,1,0:T(8,128)(2,1)S(1)}, bf16[128,128,256]{2,1,0:T(8,128)(2,1)S(1)}) custom-call(s32[1,128]{1,0:T(1,128)} %bitcast.21, s32[1,128]{1,0:T(1,128)} %bitcast.22, f32[1,128]{1,0:T(1,128)} %constant.2.clone.freq_hbm, bf16[128,2048]{1,0:T(8,128)(2,1)} %get-tuple-element.22.h_hbm, ...), custom_call_target="tpu_custom_call" | custom-call | tf_op jit(solution)/shard_map/layer1/pallas_call | solution.py:324
  75.1 6.2 %write1.1 = (bf16[2,128,128,256]{3,2,1,0:T(8,128)(2,1)}, bf16[2,128,128,256]{3,2,1,0:T(8,128)(2,1)}, bf16[128,2048]{1,0:T(8,128)(2,1)}) custom-call(bf16[128,128,256]{2,1,0:T(8,128)(2,1)S(1)} %get-tuple-element.23.refs_0_, bf16[128,128,256]{2,1,0:T(8,128)(2,1)S(1)} %get-tuple-element.24.refs_1_, ...), custom_call_target="tpu_custom_call", output_to_operand_aliasing={{0}: (3, {}), {1}: (4, {})} | custom-call | tf_op jit(solution)/shard_map/write1/pallas_call | solution.py:387

commit v8 on v7

--- a/solution.py
+++ b/solution.py
@@ -58,10 +58,25 @@
     return slab * cos + other * sin
 
 
-def layer_kernel(layer, seq_hbm, seqv_hbm, freq_hbm, h_hbm, ga_hbm, gm_hbm, wq_hbm, wk_hbm, wv_hbm, wo_hbm, wg_hbm, wu_hbm,
-                 wd_hbm, k_hbm, v_hbm, out_ref, kbuf, vbuf, seq_ref, seqv, freq, h_ref, ga, gm, wq, wk, wv, wo, wg, wu, wd,
-                 knew, vnew, krow, vrow, qrow, orow, own1, send1, recv1, pair1, peer1, mid, send2, recv2, pair2, peer2, last, act,
-                 sem, ksem, vsem, osem, wsem, sems1, sems2):
+def layer_kernel(layer, first, last, *refs):
+    (seq_hbm, seqv_hbm, freq_hbm, h_in, ga_hbm, gm_hbm, wq_in, wk_in, wv_in, wo_hbm, wg_hbm, wu_hbm, wd_hbm, k_hbm, v_hbm) = refs[:15]
+    refs = refs[15:]
+    if not first:
+        h_ref, wq, wk, wv = h_in, wq_in, wk_in, wv_in
+    if not last:
+        nq_hbm, nk_hbm, nv_hbm = (wq_in, wk_in, wv_in) if first else refs[:3]
+        refs = refs if first else refs[3:]
+    out_ref, kbuf, vbuf = refs[:3]
+    refs = refs[3:]
+    if not last:
+        next_q, next_k, next_v = refs[:3]
+        refs = refs[3:]
+    if first:
+        h_ref, wq, wk, wv = refs[:4]
+        refs = refs[4:]
+    (seq_ref, seqv, freq, ga, gm, wo, wg, wu, wd,
+     knew, vnew, krow, vrow, qrow, orow, own1, send1, recv1, pair1, peer1, mid, send2, recv2, pair2, peer2, last2, act,
+     sem, ksem, vsem, osem, wsem, nsem, sems1, sems2) = refs
     me = lax.axis_index("tp")
     core = lax.rem(me, 2)
     sibling = me + 1 - 2 * core
@@ -71,10 +86,27 @@
     for other in (sibling, peer):
         pl.semaphore_signal(barrier, inc=1, device_id={"tp": other}, device_id_type=MESH)
 
-    def small(i):
-        src, dst = ((seqv_hbm, seqv), (freq_hbm, freq), (h_hbm, h_ref), (ga_hbm, ga), (wk_hbm.at[layer], wk),
-                    (wv_hbm.at[layer], wv), (wq_hbm.at[layer], wq), (seq_hbm, seq_ref), (gm_hbm, gm))[i]
-        return pltpu.make_async_copy(src, dst, sem.at[i])
+    smalls = {0: (seqv_hbm, seqv), 1: (freq_hbm, freq), 3: (ga_hbm, ga), 7: (seq_hbm, seq_ref), 8: (gm_hbm, gm)}
+    if first:
+        smalls.update({2: (h_in, h_ref), 4: (wk_in.at[layer], wk), 5: (wv_in.at[layer], wv), 6: (wq_in.at[layer], wq)})
+
+    class Small:
+        def __init__(self, i):
+            self.copy = pltpu.make_async_copy(*smalls[i], sem.at[i]) if i in smalls else None
+
+        def start(self):
+            if self.copy is not None:
+                self.copy.start()
+
+        def wait(self):
+            if self.copy is not None:
+                self.copy.wait()
+
+    small = Small
+
+    def load_next(i):
+        src, dst = ((nq_hbm, next_q), (nk_hbm, next_k), (nv_hbm, next_v))[i]
+        return pltpu.make_async_copy(src.at[layer + 1], dst, nsem.at[i])
 
     def load_k(i):
         return pltpu.make_async_copy(k_hbm.at[layer, pl.ds(i * SEQS, SEQS)], kbuf.at[pl.ds(i * SEQS, SEQS)], ksem.at[i])
@@ -132,7 +164,6 @@
             qrow[pl.ds(hg, ROWS, stride=8), :] = jnp.where(lane // HEAD == kv, slab if kv == half else turned, 0.0)
     small(7).wait()
     small(8).wait()
-    pl.semaphore_wait(barrier, 2)
 
     def attend(i):
         load_k(i).wait()
@@ -228,6 +259,7 @@
         @pl.when(rc == 0)
         def _():
             load_o().wait()
+            pl.semaphore_wait(barrier, 2)
 
         send1[rc] = jnp.dot(attn, wo[:, half_cols(1 - core)], preferred_element_type=F32).astype(BF16)
         copy1(rc).start()
@@ -248,6 +280,9 @@
     lax.fori_loop(0, NRC, row_chunk, 0)
     for j in range(NCH):
         load(2, j).start()
+    if not last:
+        for i in range(3):
+            load_next(i).start()
     lax.fori_loop(0, 1, insert, 0)
     to_peer1(NRC - 1)
     lax.fori_loop(1, STEPS, insert, 0)
@@ -279,7 +314,7 @@
         return remote(pair2.at[j], peer2.at[j], sems2, 1, j, peer)
 
     def copy2_out(j, half):
-        return remote(last.at[half * 2 + j], last.at[half * 2 + j], sems2, 2, j, sibling)
+        return remote(last2.at[half * 2 + j], last2.at[half * 2 + j], sems2, 2, j, sibling)
 
     def down(j):
         return jnp.dot(act[...], wd[:, pl.ds(pl.multiple_of(j * CW, CW), CW)], preferred_element_type=F32)
@@ -301,12 +336,15 @@
     for j in range(2):
         copy2_peer(j).wait_recv()
         total = pair2[j].astype(F32) + peer2[j].astype(F32)
-        last[core * 2 + j] = (mid[core, :, j * CW:(j + 1) * CW].astype(F32) + total).astype(BF16)
+        last2[core * 2 + j] = (mid[core, :, j * CW:(j + 1) * CW].astype(F32) + total).astype(BF16)
         copy2_out(j, core).start()
     for j in range(2):
         copy2_out(j, 1 - core).wait_recv()
     for j in range(NCH):
-        out_ref[:, j * CW:(j + 1) * CW] = last[j]
+        out_ref[:, j * CW:(j + 1) * CW] = last2[j]
+    if not last:
+        for i in range(3):
+            load_next(i).wait()
     for rc in range(NRC):
         copy1(rc).wait_send()
         copy1_peer(rc).wait_send()
@@ -317,25 +355,26 @@
         copy2_out(j, core).wait_send()
 
 
-def layer_call(layer, last, seq_lens, freq, hidden, g_attn, g_mlp, w_q, w_k, w_v, w_o, w_gate, w_up, w_down, k_cache, v_cache):
+def layer_call(layer, first, last, seq_lens, freq, hidden, g_attn, g_mlp, qkv, w_next, w_o, w_gate, w_up, w_down, k_cache, v_cache):
     tile = pltpu.VMEM((ROWS, KVD, SMAX), BF16)
     chunk1 = pltpu.VMEM((NRC, RC, HALF), BF16)
     chunk2 = pltpu.VMEM((2, ROWS, CW), BF16)
+    weights = [pltpu.VMEM((D, QD), BF16), pltpu.VMEM((D, KVD), BF16), pltpu.VMEM((D, KVD), BF16)]
+    space = pltpu.HBM if first else pltpu.VMEM
+    near = HBM if first else VMEM
+    hidden, *qkv = (pltpu.with_memory_space_constraint(x, space) for x in (hidden, *qkv))
+    handed = [] if last or first else list(w_next)
     return pl.pallas_call(
-        functools.partial(layer_kernel, layer),
-        out_shape=(pltpu.VMEM((ROWS, D), BF16) if last else jax.ShapeDtypeStruct((ROWS, D), BF16), tile, tile),
-        in_specs=[HBM] * 15,
-        out_specs=(VMEM, VMEM, VMEM),
-        scratch_shapes=[
+        functools.partial(layer_kernel, layer, first, last),
+        out_shape=[pltpu.VMEM((ROWS, D), BF16), tile, tile] + ([] if last else weights),
+        in_specs=[HBM] * 3 + [near] + [HBM] * 2 + [near] * 3 + [HBM] * (6 + len(handed)),
+        out_specs=[VMEM] * (3 if last else 6),
+        scratch_shapes=([pltpu.VMEM((ROWS, D), BF16)] + weights if first else []) + [
             pltpu.SMEM((1, ROWS), jnp.int32),
             pltpu.VMEM((1, ROWS), jnp.int32),
             pltpu.VMEM((1, 128), F32),
-            pltpu.VMEM((ROWS, D), BF16),
             pltpu.VMEM(g_attn.shape, BF16),
             pltpu.VMEM(g_mlp.shape, BF16),
-            pltpu.VMEM((D, QD), BF16),
-            pltpu.VMEM((D, KVD), BF16),
-            pltpu.VMEM((D, KVD), BF16),
             pltpu.VMEM((QD, D), BF16),
             pltpu.VMEM((D, FF), BF16),
             pltpu.VMEM((D, FF), BF16),
@@ -357,12 +396,13 @@
             pltpu.SemaphoreType.DMA((STEPS,)),
             pltpu.SemaphoreType.DMA((1,)),
             pltpu.SemaphoreType.DMA((3, NCH)),
+            pltpu.SemaphoreType.DMA((3,)),
             pltpu.SemaphoreType.DMA((6, NRC)),
             pltpu.SemaphoreType.DMA((6, 2)),
         ],
-        compiler_params=pltpu.CompilerParams(vmem_limit_bytes=44 * 2 ** 20, collective_id=layer, has_side_effects=True),
+        compiler_params=pltpu.CompilerParams(vmem_limit_bytes=(38 if first else 35) * 2 ** 20, collective_id=layer, has_side_effects=True),
         name=f"layer{layer}",
-    )(seq_lens, seq_lens, freq, hidden, g_attn, g_mlp, w_q, w_k, w_v, w_o, w_gate, w_up, w_down, k_cache, v_cache)
+    )(seq_lens, seq_lens, freq, hidden, g_attn, g_mlp, *qkv, w_o, w_gate, w_up, w_down, k_cache, v_cache, *handed)
 
 
 def write_kernel(layer, n_in, *refs):
@@ -414,9 +454,10 @@
             pltpu.with_memory_space_constraint(x, pltpu.HBM)
             for x in (hidden, g_attn, w_q, w_k, w_v, w_o, g_mlp, w_gate, w_up, w_down, kt, vt, freq, seq_row))
         outs = ()
+        qkv = (w_q, w_k, w_v)
         for layer in range(layers):
-            hidden, k_tile, v_tile = layer_call(layer, layer == layers - 1, seq_row, freq, hidden, g_attn, g_mlp, w_q, w_k, w_v, w_o, w_gate, w_up,
-                                                w_down, kt, vt)
+            hidden, k_tile, v_tile, *qkv = layer_call(layer, layer == 0, layer == layers - 1, seq_row, freq, hidden, g_attn, g_mlp, qkv,
+                                                      (w_q, w_k, w_v), w_o, w_gate, w_up, w_down, kt, vt)
             if layer < layers - 1:
                 outs = write_call(layer, layers, (k_tile, v_tile), outs)
                 hidden, outs = lax.optimization_barrier((hidden, outs))

time: 81.6 us -> 81.2 us (level)
  no operation moved by 1% of the time
where the time goes in v8:
time: 81.2 us; the launch traced here: 81.1 us
  Pallas kernels  80.3 us (99%)
  between operations  0.82 us (1%)
    pallas_call x2, Pallas kernels, layer_call(): pl.pallas_call(functools.partial(layer_kernel, layer, first, last), out_s...  68.1 us
    pallas_call x2, Pallas kernels, write_call(): pl.pallas_call(functools.partial(write_kernel, layer, n_in), out_shape=(c...  12.2 us

profile of v8, /device:TPU:0, one launch (start us, length us, event | category | flops | bytes accessed | tf_op | source)
XLA Modules:
  0.0 81.1 jit_solution(5253510599668333676)
XLA Ops:
  0.6 35.2 %layer0.1 = (bf16[128,2048]{1,0:T(8,128)(2,1)S(1)}, bf16[128,128,256]{2,1,0:T(8,128)(2,1)S(1)}, bf16[128,128,256]{2,1,0:T(8,128)(2,1)S(1)}, bf16[2048,512]{1,0:T...) custom-call(s32[1,128]{1,0:T(1,128)} %bitcast.19, s32[1,128]{1,0:T(1,128)} %bitcast.20, ...), custom_call_target="tpu_custom_call" | custom-call | tf_op jit(solution)/shard_map/layer0/pallas_call | solution.py:367
  35.8 6.0 %write0.1 = (bf16[2,128,128,256]{3,2,1,0:T(8,128)(2,1)}, bf16[2,128,128,256]{3,2,1,0:T(8,128)(2,1)}) custom-call(bf16[128,128,256]{2,1,0:T(8,128)(2,1)S(1)} %get-tuple-element.21.refs_0_, bf16[128,128,256]{2,1,0:T(8,128)(2,1)S(1)} %get-tuple-element.22.refs_1_), custom_call_target="tpu_custom_call" | custom-call | tf_op jit(solution)/shard_map/write0/pallas_call | solution.py:427
  41.9 32.9 %layer1.1 = (bf16[128,2048]{1,0:T(8,128)(2,1)S(1)}, bf16[128,128,256]{2,1,0:T(8,128)(2,1)S(1)}, bf16[128,128,256]{2,1,0:T(8,128)(2,1)S(1)}) custom-call(s32[1,128]{1,0:T(1,128)} %bitcast.21, s32[1,128]{1,0:T(1,128)} %bitcast.22, f32[1,128]{1,0:T(1,128)} %constant.2.clone.refs_2_, bf16[128,2048]{1,0:T(8,128)(2,1)S(1)} %get-tuple-element.25.refs_3_, ...), custom_call_target="tpu_custom_call" | custom-call | tf_op jit(solution)/shard_map/layer1/pallas_call | solution.py:367
  74.8 6.2 %write1.1 = (bf16[2,128,128,256]{3,2,1,0:T(8,128)(2,1)}, bf16[2,128,128,256]{3,2,1,0:T(8,128)(2,1)}, bf16[128,2048]{1,0:T(8,128)(2,1)}) custom-call(bf16[128,128,256]{2,1,0:T(8,128)(2,1)S(1)} %get-tuple-element.29.refs_0_, bf16[128,128,256]{2,1,0:T(8,128)(2,1)S(1)} %get-tuple-element.30.refs_1_, ...), custom_call_target="tpu_custom_call", output_to_operand_aliasing={{0}: (3, {}), {1}: (4, {})} | custom-call | tf_op jit(solution)/shard_map/write1/pallas_call | solution.py:427

commit v9 on v8

--- a/solution.py
+++ b/solution.py
@@ -244,7 +244,16 @@
 
     def row_chunk(rc, carry):
         def step(i, c):
+            @pl.when((i == RC // SEQS - 1) & (rc == 0))
+            def _():
+                pl.semaphore_wait(barrier, 2)
+
             attend(rc * (RC // SEQS) + i)
+
+            @pl.when((i == 0) & (rc > 0))
+            def _():
+                to_peer1(rc - 1)
+
             return c
 
         lax.fori_loop(0, RC // SEQS, step, 0)
@@ -259,15 +268,10 @@
         @pl.when(rc == 0)
         def _():
             load_o().wait()
-            pl.semaphore_wait(barrier, 2)
 
         send1[rc] = jnp.dot(attn, wo[:, half_cols(1 - core)], preferred_element_type=F32).astype(BF16)
         copy1(rc).start()
         own1[rc] = jnp.dot(attn, wo[:, half_cols(core)], preferred_element_type=F32)
-
-        @pl.when(rc > 0)
-        def _():
-            to_peer1(rc - 1)
 
         @pl.when(rc == NRC - 2)
         def _():
@@ -283,9 +287,7 @@
     if not last:
         for i in range(3):
             load_next(i).start()
-    lax.fori_loop(0, 1, insert, 0)
     to_peer1(NRC - 1)
-    lax.fori_loop(1, STEPS, insert, 0)
     for rc in range(NRC):
         copy1_peer(rc).wait_recv()
         total = pair1[rc].astype(F32) + peer1[rc].astype(F32)
@@ -333,6 +335,7 @@
     to_sibling2(1)
     to_peer2(0, own)
     to_peer2(1, down(core * 2 + 1))
+    lax.fori_loop(0, STEPS, insert, 0)
     for j in range(2):
         copy2_peer(j).wait_recv()
         total = pair2[j].astype(F32) + peer2[j].astype(F32)

time: 81.2 us -> 78.1 us (0.962)
  Pallas kernels: 80.3 us -> 77.1 us
    pallas_call x2, Pallas kernels: 68.1 us -> 64.9 us  [layer_call(): pl.pallas_call(functools.partial(layer_kernel, layer, first, last), out_s...]
where the time goes in v9:
time: 78.1 us; the launch traced here: 77.9 us
  Pallas kernels  77.1 us (99%)
  between operations  0.82 us (1%)
    pallas_call x2, Pallas kernels, layer_call(): pl.pallas_call(functools.partial(layer_kernel, layer, first, last), out_s...  64.9 us
    pallas_call x2, Pallas kernels, write_call(): pl.pallas_call(functools.partial(write_kernel, layer, n_in), out_shape=(c...  12.2 us

profile of v9, /device:TPU:0, one launch (start us, length us, event | category | flops | bytes accessed | tf_op | source)
XLA Modules:
  0.0 77.9 jit_solution(7588936883601906234)
XLA Ops:
  0.6 32.9 %layer0.1 = (bf16[128,2048]{1,0:T(8,128)(2,1)S(1)}, bf16[128,128,256]{2,1,0:T(8,128)(2,1)S(1)}, bf16[128,128,256]{2,1,0:T(8,128)(2,1)S(1)}, bf16[2048,512]{1,0:T...) custom-call(s32[1,128]{1,0:T(1,128)} %bitcast.19, s32[1,128]{1,0:T(1,128)} %bitcast.20, ...), custom_call_target="tpu_custom_call" | custom-call | tf_op jit(solution)/shard_map/layer0/pallas_call | solution.py:370
  33.6 6.0 %write0.1 = (bf16[2,128,128,256]{3,2,1,0:T(8,128)(2,1)}, bf16[2,128,128,256]{3,2,1,0:T(8,128)(2,1)}) custom-call(bf16[128,128,256]{2,1,0:T(8,128)(2,1)S(1)} %get-tuple-element.21.refs_0_, bf16[128,128,256]{2,1,0:T(8,128)(2,1)S(1)} %get-tuple-element.22.refs_1_), custom_call_target="tpu_custom_call" | custom-call | tf_op jit(solution)/shard_map/write0/pallas_call | solution.py:430
  39.6 32.0 %layer1.1 = (bf16[128,2048]{1,0:T(8,128)(2,1)S(1)}, bf16[128,128,256]{2,1,0:T(8,128)(2,1)S(1)}, bf16[128,128,256]{2,1,0:T(8,128)(2,1)S(1)}) custom-call(s32[1,128]{1,0:T(1,128)} %bitcast.21, s32[1,128]{1,0:T(1,128)} %bitcast.22, f32[1,128]{1,0:T(1,128)} %constant.2.clone.refs_2_, bf16[128,2048]{1,0:T(8,128)(2,1)S(1)} %get-tuple-element.25.refs_3_, ...), custom_call_target="tpu_custom_call" | custom-call | tf_op jit(solution)/shard_map/layer1/pallas_call | solution.py:370
  71.6 6.2 %write1.1 = (bf16[2,128,128,256]{3,2,1,0:T(8,128)(2,1)}, bf16[2,128,128,256]{3,2,1,0:T(8,128)(2,1)}, bf16[128,2048]{1,0:T(8,128)(2,1)}) custom-call(bf16[128,128,256]{2,1,0:T(8,128)(2,1)S(1)} %get-tuple-element.29.refs_0_, bf16[128,128,256]{2,1,0:T(8,128)(2,1)S(1)} %get-tuple-element.30.refs_1_, ...), custom_call_target="tpu_custom_call", output_to_operand_aliasing={{0}: (3, {}), {1}: (4, {})} | custom-call | tf_op jit(solution)/shard_map/write1/pallas_call | solution.py:430

commit v10 on v9

--- a/solution.py
+++ b/solution.py
@@ -29,7 +29,7 @@
 HALF = D // 2
 RC = 32
 NRC = ROWS // RC
-AHEAD = 3
+AHEAD = 4
 F32 = jnp.float32
 BF16 = jnp.bfloat16
 MESH = pl.DeviceIdType.MESH
@@ -249,11 +249,6 @@
                 pl.semaphore_wait(barrier, 2)
 
             attend(rc * (RC // SEQS) + i)
-
-            @pl.when((i == 0) & (rc > 0))
-            def _():
-                to_peer1(rc - 1)
-
             return c
 
         lax.fori_loop(0, RC // SEQS, step, 0)
@@ -271,6 +266,11 @@
 
         send1[rc] = jnp.dot(attn, wo[:, half_cols(1 - core)], preferred_element_type=F32).astype(BF16)
         copy1(rc).start()
+
+        @pl.when(rc > 0)
+        def _():
+            to_peer1(rc - 1)
+
         own1[rc] = jnp.dot(attn, wo[:, half_cols(core)], preferred_element_type=F32)
 
         @pl.when(rc == NRC - 2)

time: 78.1 us -> 80.1 us (1.026)
  Pallas kernels: 77.1 us -> 79.2 us
    pallas_call x2, Pallas kernels: 64.9 us -> 67 us  [layer_call(): pl.pallas_call(functools.partial(layer_kernel, layer, first, last), out_s...]
where the time goes in v10:
time: 80.1 us; the launch traced here: 80 us
  Pallas kernels  79.2 us (99%)
  between operations  0.82 us (1%)
    pallas_call x2, Pallas kernels, layer_call(): pl.pallas_call(functools.partial(layer_kernel, layer, first, last), out_s...  67 us
    pallas_call x2, Pallas kernels, write_call(): pl.pallas_call(functools.partial(write_kernel, layer, n_in), out_shape=(c...  12.2 us

profile of v10, /device:TPU:0, one launch (start us, length us, event | category | flops | bytes accessed | tf_op | source)
XLA Modules:
  0.0 80.0 jit_solution(1913666376055336681)
XLA Ops:
  0.6 33.8 %layer0.1 = (bf16[128,2048]{1,0:T(8,128)(2,1)S(1)}, bf16[128,128,256]{2,1,0:T(8,128)(2,1)S(1)}, bf16[128,128,256]{2,1,0:T(8,128)(2,1)S(1)}, bf16[2048,512]{1,0:T...) custom-call(s32[1,128]{1,0:T(1,128)} %bitcast.19, s32[1,128]{1,0:T(1,128)} %bitcast.20, ...), custom_call_target="tpu_custom_call" | custom-call | tf_op jit(solution)/shard_map/layer0/pallas_call | solution.py:370
  34.4 6.0 %write0.1 = (bf16[2,128,128,256]{3,2,1,0:T(8,128)(2,1)}, bf16[2,128,128,256]{3,2,1,0:T(8,128)(2,1)}) custom-call(bf16[128,128,256]{2,1,0:T(8,128)(2,1)S(1)} %get-tuple-element.21.refs_0_, bf16[128,128,256]{2,1,0:T(8,128)(2,1)S(1)} %get-tuple-element.22.refs_1_), custom_call_target="tpu_custom_call" | custom-call | tf_op jit(solution)/shard_map/write0/pallas_call | solution.py:430
  40.5 33.2 %layer1.1 = (bf16[128,2048]{1,0:T(8,128)(2,1)S(1)}, bf16[128,128,256]{2,1,0:T(8,128)(2,1)S(1)}, bf16[128,128,256]{2,1,0:T(8,128)(2,1)S(1)}) custom-call(s32[1,128]{1,0:T(1,128)} %bitcast.21, s32[1,128]{1,0:T(1,128)} %bitcast.22, f32[1,128]{1,0:T(1,128)} %constant.2.clone.refs_2_, bf16[128,2048]{1,0:T(8,128)(2,1)S(1)} %get-tuple-element.25.refs_3_, ...), custom_call_target="tpu_custom_call" | custom-call | tf_op jit(solution)/shard_map/layer1/pallas_call | solution.py:370
  73.7 6.2 %write1.1 = (bf16[2,128,128,256]{3,2,1,0:T(8,128)(2,1)}, bf16[2,128,128,256]{3,2,1,0:T(8,128)(2,1)}, bf16[128,2048]{1,0:T(8,128)(2,1)}) custom-call(bf16[128,128,256]{2,1,0:T(8,128)(2,1)S(1)} %get-tuple-element.29.refs_0_, bf16[128,128,256]{2,1,0:T(8,128)(2,1)S(1)} %get-tuple-element.30.refs_1_, ...), custom_call_target="tpu_custom_call", output_to_operand_aliasing={{0}: (3, {}), {1}: (4, {})} | custom-call | tf_op jit(solution)/shard_map/write1/pallas_call | solution.py:430

commit v11 on v9

--- a/solution.py
+++ b/solution.py
@@ -144,9 +144,8 @@
     normed = norm_rows(h_ref[...].astype(F32), ga[layer:layer + 1, :])
     small(4).wait()
     small(5).wait()
-    for i in range(1, AHEAD):
-        load_k(i).start()
-        load_v(i).start()
+    load_k(1).start()
+    load_v(1).start()
     k_row = rope_slab(jnp.dot(normed, wk[...], preferred_element_type=F32), cos, sin).astype(BF16).astype(F32)
     v_row = jnp.dot(normed, wv[...], preferred_element_type=F32).astype(BF16).astype(F32)
     krow[...] = k_row
@@ -169,14 +168,17 @@
         load_k(i).wait()
         load_v(i).wait()
 
+        @pl.when(i == 0)
+        def _():
+            load_o().start()
+            for n in range(2, AHEAD):
+                load_k(n).start()
+                load_v(n).start()
+
         @pl.when(i + AHEAD < STEPS)
         def _():
             load_k(i + AHEAD).start()
             load_v(i + AHEAD).start()
-
-        @pl.when(i == 0)
-        def _():
-            load_o().start()
 
         lane8 = lax.broadcasted_iota(jnp.int32, (8, SMAX), 1)
         row16 = lax.broadcasted_iota(jnp.int32, (16, 128), 0)

time: 78.1 us -> 78.6 us (level)
  no operation moved by 1% of the time
where the time goes in v11:
time: 78.6 us; the launch traced here: 78.5 us
  Pallas kernels  77.7 us (99%)
  between operations  0.82 us (1%)
    pallas_call x2, Pallas kernels, layer_call(): pl.pallas_call(functools.partial(layer_kernel, layer, first, last), out_s...  65.4 us
    pallas_call x2, Pallas kernels, write_call(): pl.pallas_call(functools.partial(write_kernel, layer, n_in), out_shape=(c...  12.2 us

profile of v11, /device:TPU:0, one launch (start us, length us, event | category | flops | bytes accessed | tf_op | source)
XLA Modules:
  0.0 78.5 jit_solution(4154441804208727169)
XLA Ops:
  0.6 33.5 %layer0.1 = (bf16[128,2048]{1,0:T(8,128)(2,1)S(1)}, bf16[128,128,256]{2,1,0:T(8,128)(2,1)S(1)}, bf16[128,128,256]{2,1,0:T(8,128)(2,1)S(1)}, bf16[2048,512]{1,0:T...) custom-call(s32[1,128]{1,0:T(1,128)} %bitcast.19, s32[1,128]{1,0:T(1,128)} %bitcast.20, ...), custom_call_target="tpu_custom_call" | custom-call | tf_op jit(solution)/shard_map/layer0/pallas_call | solution.py:372
  34.1 6.0 %write0.1 = (bf16[2,128,128,256]{3,2,1,0:T(8,128)(2,1)}, bf16[2,128,128,256]{3,2,1,0:T(8,128)(2,1)}) custom-call(bf16[128,128,256]{2,1,0:T(8,128)(2,1)S(1)} %get-tuple-element.21.refs_0_, bf16[128,128,256]{2,1,0:T(8,128)(2,1)S(1)} %get-tuple-element.22.refs_1_), custom_call_target="tpu_custom_call" | custom-call | tf_op jit(solution)/shard_map/write0/pallas_call | solution.py:432
  40.2 32.0 %layer1.1 = (bf16[128,2048]{1,0:T(8,128)(2,1)S(1)}, bf16[128,128,256]{2,1,0:T(8,128)(2,1)S(1)}, bf16[128,128,256]{2,1,0:T(8,128)(2,1)S(1)}) custom-call(s32[1,128]{1,0:T(1,128)} %bitcast.21, s32[1,128]{1,0:T(1,128)} %bitcast.22, f32[1,128]{1,0:T(1,128)} %constant.2.clone.refs_2_, bf16[128,2048]{1,0:T(8,128)(2,1)S(1)} %get-tuple-element.25.refs_3_, ...), custom_call_target="tpu_custom_call" | custom-call | tf_op jit(solution)/shard_map/layer1/pallas_call | solution.py:372
  72.1 6.2 %write1.1 = (bf16[2,128,128,256]{3,2,1,0:T(8,128)(2,1)}, bf16[2,128,128,256]{3,2,1,0:T(8,128)(2,1)}, bf16[128,2048]{1,0:T(8,128)(2,1)}) custom-call(bf16[128,128,256]{2,1,0:T(8,128)(2,1)S(1)} %get-tuple-element.29.refs_0_, bf16[128,128,256]{2,1,0:T(8,128)(2,1)S(1)} %get-tuple-element.30.refs_1_, ...), custom_call_target="tpu_custom_call", output_to_operand_aliasing={{0}: (3, {}), {1}: (4, {})} | custom-call | tf_op jit(solution)/shard_map/write1/pallas_call | solution.py:432
